TPU v7x, 256 devices: a whole 4x4x8 slice. The times are simulated.
256 devices in a mesh: nx: 8 (over x, core), ny: 16 (over y_lo, z), img: 2 (over y_hi).
Axes of the slice: x: 4, y: 4 (y_hi: 2, y_lo: 2; y = y_hi * 2 + y_lo), z: 8, core: 2. Of those that a mesh axis runs over, the one named last changes fastest.
Arguments:
- features: bfloat16 [256, 65536], P(('nx', 'ny', 'img')), may hold values from 0 to 2
- link_weight: bfloat16 [3, 128, 128, 128, 128], P(None, ('nx', 'ny')), may hold values from -0.1875 to 0.1875
- link_row: int32 [3, 128, 128], P(None, ('nx', 'ny')), may hold values from 0 to 3
- link_col: int32 [3, 128, 128], P(None, None, ('nx', 'ny')), may hold values from 0 to 3
- link_live: int32 [3, 128, 128], P(None, ('nx', 'ny')), may hold values from 0 to 1, as said below
- bias: float32 [3, 65536], P(None, ('nx', 'ny')), may hold values from -3 to 3
Outputs:
- activations: bfloat16 [256, 65536], P(('nx', 'ny', 'img'))
Inputs may be any that keep to these rules, and one draw needn't show every extreme that they name: `link_live`: in every layer at most 96 of the links of one source device are live, and exactly 96 for some source device.
All inputs are finite; a program needn't handle non-finite values.
Results may differ from a plain program's by a relative error of at most 0.0072.
Values may be sent and summed in bfloat16 or wider, within the bound.
A program may use at most 64 MiB of HBM per device.

v0:
```python
import jax
import jax.numpy as jnp
from jax import lax
from jax.sharding import PartitionSpec as P


def combine_links(received, col_ids, width):
    onehot = (col_ids[:, None] == jnp.arange(width, dtype=jnp.int32)[None, :]).astype(jnp.bfloat16)
    summed = jnp.einsum("dq,dis->iqs", onehot, received, preferred_element_type=jnp.float32)
    return summed.reshape(summed.shape[0], width * received.shape[2])


def link_products(blocks, weights, row_ids, live_mask):
    masked = weights * live_mask.astype(jnp.bfloat16)[:, None, None]
    gathered = jnp.take(blocks, row_ids, axis=1)
    result = jnp.einsum(
        "ier,ers->eis", gathered, masked, preferred_element_type=jnp.float32
    ).astype(jnp.bfloat16)
    return result


def local(features, link_weight, link_row, link_col, link_live, bias):
    block_size = link_weight.shape[-1]
    width = bias.shape[1] // block_size
    hidden = lax.all_to_all(features, ("nx", "ny"), split_axis=1, concat_axis=0, tiled=True)
    image_rows = hidden.shape[0]
    for layer_idx in range(bias.shape[0]):
        blocks = hidden.reshape(image_rows, width, block_size)
        link_terms = link_products(
            blocks, link_weight[layer_idx, 0], link_row[layer_idx, 0], link_live[layer_idx, 0]
        )
        col_ids = link_col[layer_idx, :, 0]
        summed = combine_links(
            lax.all_to_all(link_terms, ("nx", "ny"), split_axis=0, concat_axis=0, tiled=True),
            col_ids,
            width,
        )
        hidden = jnp.maximum(summed + bias[layer_idx][None, :], 0.0).astype(jnp.bfloat16)
    finished = lax.all_to_all(hidden, ("nx", "ny"), split_axis=0, concat_axis=1, tiled=True)
    return finished


def solution(mesh):
    placed = (
        P(("nx", "ny", "img"), None),
        P(None, ("nx", "ny"), None, None, None),
        P(None, ("nx", "ny"), None),
        P(None, None, ("nx", "ny")),
        P(None, ("nx", "ny"), None),
        P(None, ("nx", "ny")),
    )
    return jax.shard_map(
        local, mesh=mesh, in_specs=placed, out_specs=P(("nx", "ny", "img"), None), check_vma=False
    )
```

profile of v0, /device:TPU:1, one launch (start us, length us, event | category | flops | bytes accessed | tf_op | source)
XLA Modules:
  0.0 399.7 jit_solution(4296205948690893251)
XLA Ops:
  0.0 0.5 broadcast.102
  0.5 2.3 reduce
  2.8 0.7 reshape.137
  3.5 14.8 %all-to-all-start = ((bf16[128,2,256]{2,1,0:T(2,128)(2,1)}), bf16[128,2,256]{2,1,0:T(2,128)(2,1)S(1)}, u32[]{:S(2)}, u32[]{:S(2)}) async-start(bf16[128,2,256]{2,1,0:T(2,128)(2,1)} %reshape.137), calls=%async_computation | async-start | bytes 262144 | tf_op jit(solution)/shard_map/all_to_all | solution.py:25
  18.3 0.7 compare_and_fusion
  19.0 0.7 convert.5
  19.7 9.6 %all-to-all-done = bf16[128,2,256]{2,1,0:T(2,128)(2,1)S(1)} async-done(((bf16[128,2,256]{2,1,0:T(2,128)(2,1)}), bf16[128,2,256]{2,1,0:T(2,128)(2,1)S(1)}, u32[]{:S(2)}, u32[]{:S(2)}) %all-to-all-start) | async-done | bytes 131104 | tf_op jit(solution)/shard_map/all_to_all | solution.py:25
  29.3 0.1 reshape.138
  29.5 0.2 copy.32
  29.6 0.1 copy.33
  29.8 3.1 gather_fusion
  32.8 6.7 %fusion.21 = bf16[128,128,128]{2,1,0:T(8,128)(2,1)} fusion(bf16[3,1,128,128,128]{4,3,2,1,0:T(8,128)(2,1)} %param.9, bf16[128,128,128]{2,1,0:T(8,128)(2,1)} %gather_fusion, pred[128]{0:T(512)(128)(4,1)S(1)} %get-tuple-element.21, bf16[128]{0:T(256)(128)(2,1)S(1)} %get-tuple-element.20), kind=kOutput, calls=%fused_computation.27 | convolution fusion | flops 543162368 | bytes 12583296 | tf_op jit(solution)/shard_map/ier,ers->eis/dot_general | solution.py:16
  39.6 0.0 copy-start.1
  39.6 0.0 copy-start
  39.6 7.9 %all-to-all-start.1 = ((bf16[128,128,128]{2,1,0:T(8,128)(2,1)}), bf16[128,128,128]{2,1,0:T(8,128)(2,1)}, u32[]{:S(2)}, u32[]{:S(2)}) async-start(bf16[128,128,128]{2,1,0:T(8,128)(2,1)} %fusion.21), calls=%async_computation.1 | async-start | bytes 8388608 | tf_op jit(solution)/shard_map/all_to_all | solution.py:34
  47.4 0.0 copy-done.1
  47.5 0.0 copy-done
  47.5 96.0 %all-to-all-done.1 = bf16[128,128,128]{2,1,0:T(8,128)(2,1)} async-done(((bf16[128,128,128]{2,1,0:T(8,128)(2,1)}), bf16[128,128,128]{2,1,0:T(8,128)(2,1)}, u32[]{:S(2)}, u32[]{:S(2)}) %all-to-all-start.1) | async-done | bytes 4194336 | tf_op jit(solution)/shard_map/all_to_all | solution.py:34
  143.5 4.5 %fusion.57 = bf16[128,4,128]{2,1,0:T(4,128)(2,1)S(1)} fusion(bf16[128,128,128]{2,1,0:T(8,128)(2,1)} %all-to-all-done.1, f32[4,128]{1,0:T(4,128)S(1)} %bitcast.91, s32[128]{0:T(128)S(1)} %get-tuple-element.16), kind=kOutput, calls=%fused_computation.43 | convolution fusion | flops 16974336 | bytes 4327936 | tf_op jit(solution)/shard_map/dq,dis->iqs/dot_general | solution.py:9
  148.0 3.1 gather_fusion.1
  151.1 6.7 %fusion.24 = bf16[128,128,128]{2,1,0:T(8,128)(2,1)} fusion(bf16[3,1,128,128,128]{4,3,2,1,0:T(8,128)(2,1)} %param.9, bf16[128,128,128]{2,1,0:T(8,128)(2,1)} %gather_fusion.1, pred[128]{0:T(512)(128)(4,1)S(1)} %get-tuple-element.23, bf16[128]{0:T(256)(128)(2,1)S(1)} %get-tuple-element.19), kind=kOutput, calls=%fused_computation.28 | convolution fusion | flops 543162368 | bytes 12583296 | tf_op jit(solution)/shard_map/ier,ers->eis/dot_general | solution.py:16
  157.8 8.6 %all-to-all-start.2 = ((bf16[128,128,128]{2,1,0:T(8,128)(2,1)}), bf16[128,128,128]{2,1,0:T(8,128)(2,1)}, u32[]{:S(2)}, u32[]{:S(2)}) async-start(bf16[128,128,128]{2,1,0:T(8,128)(2,1)} %fusion.24), calls=%async_computation.2 | async-start | bytes 8388608 | tf_op jit(solution)/shard_map/all_to_all | solution.py:34
  166.5 96.0 %all-to-all-done.2 = bf16[128,128,128]{2,1,0:T(8,128)(2,1)} async-done(((bf16[128,128,128]{2,1,0:T(8,128)(2,1)}), bf16[128,128,128]{2,1,0:T(8,128)(2,1)}, u32[]{:S(2)}, u32[]{:S(2)}) %all-to-all-start.2) | async-done | bytes 4194336 | tf_op jit(solution)/shard_map/all_to_all | solution.py:34
  262.5 4.5 %fusion.60 = bf16[128,4,128]{2,1,0:T(4,128)(2,1)S(1)} fusion(bf16[128,128,128]{2,1,0:T(8,128)(2,1)} %all-to-all-done.2, f32[4,128]{1,0:T(4,128)S(1)} %bitcast.90, s32[128]{0:T(128)S(1)} %get-tuple-element.17), kind=kOutput, calls=%fused_computation.44 | convolution fusion | flops 16974336 | bytes 4327936 | tf_op jit(solution)/shard_map/dq,dis->iqs/dot_general | solution.py:9
  267.1 3.0 gather_fusion.2
  270.1 4.8 %fusion.27 = bf16[128,128,128]{2,1,0:T(8,128)(2,1)S(1)} fusion(bf16[3,1,128,128,128]{4,3,2,1,0:T(8,128)(2,1)} %param.9, bf16[128,128,128]{2,1,0:T(8,128)(2,1)} %gather_fusion.2, pred[128]{0:T(512)(128)(4,1)S(1)} %get-tuple-element.6, bf16[128]{0:T(256)(128)(2,1)S(1)} %get-tuple-element.18), kind=kOutput, calls=%fused_computation.29 | convolution fusion | flops 543162368 | bytes 12583296 | tf_op jit(solution)/shard_map/ier,ers->eis/dot_general | solution.py:16
  274.9 103.1 %all_to_all.41 = bf16[128,128,128]{2,1,0:T(8,128)(2,1)S(1)} all-to-all(bf16[128,128,128]{2,1,0:T(8,128)(2,1)S(1)} %fusion.27), channel_id=1, replica_groups=mesh['nx'=8,'ny'=16,'img'=2] {'nx','ny'}, dimensions={0} | all-to-all | bytes 8388608 | tf_op jit(solution)/shard_map/all_to_all | solution.py:34
  378.0 2.3 fusion.48
  380.3 0.1 reshape.100
  380.5 0.7 reduce.1
  381.2 17.7 %all_to_all.42 = bf16[128,2,256]{2,1,0:T(2,128)(2,1)S(1)} all-to-all(bf16[128,2,256]{2,1,0:T(2,128)(2,1)S(1)} %reshape.139), channel_id=1, replica_groups=mesh['nx'=8,'ny'=16,'img'=2] {'nx','ny'}, dimensions={0} | all-to-all | bytes 262144 | tf_op jit(solution)/shard_map/all_to_all | solution.py:39
  398.9 0.8 reshape.140
  (10 shorter events, 0.1 us)
Async XLA Ops:
  3.5 25.8 %all-to-all-start = ((bf16[128,2,256]{2,1,0:T(2,128)(2,1)}), bf16[128,2,256]{2,1,0:T(2,128)(2,1)S(1)}, u32[]{:S(2)}, u32[]{:S(2)}) async-start(bf16[128,2,256]{2,1,0:T(2,128)(2,1)} %reshape.137), calls=%async_computation | async-start | bytes 262144 | tf_op jit(solution)/shard_map/all_to_all | solution.py:25
  39.6 7.9 %copy-start.1 = (s32[3,128,1]{1,2,0:T(1,128)S(1)}, s32[3,128,1]{1,2,0:T(1,128)}, u32[]{:S(2)}) copy-start(s32[3,128,1]{1,2,0:T(1,128)} %param.11) | copy-start | bytes 4612
  39.6 7.9 %copy-start = (f32[3,512]{1,0:T(4,128)S(1)}, f32[3,512]{1,0:T(4,128)}, u32[]{:S(2)}) copy-start(f32[3,512]{1,0:T(4,128)} %param.13) | copy-start | bytes 18436
  39.6 103.9 %all-to-all-start.1 = ((bf16[128,128,128]{2,1,0:T(8,128)(2,1)}), bf16[128,128,128]{2,1,0:T(8,128)(2,1)}, u32[]{:S(2)}, u32[]{:S(2)}) async-start(bf16[128,128,128]{2,1,0:T(8,128)(2,1)} %fusion.21), calls=%async_computation.1 | async-start | bytes 8388608 | tf_op jit(solution)/shard_map/all_to_all | solution.py:34
  157.8 104.7 %all-to-all-start.2 = ((bf16[128,128,128]{2,1,0:T(8,128)(2,1)}), bf16[128,128,128]{2,1,0:T(8,128)(2,1)}, u32[]{:S(2)}, u32[]{:S(2)}) async-start(bf16[128,128,128]{2,1,0:T(8,128)(2,1)} %fusion.24), calls=%async_computation.2 | async-start | bytes 8388608 | tf_op jit(solution)/shard_map/all_to_all | solution.py:34
where the time goes:
time: 400 us
  waiting for transfers between devices  202 us (50%)
  blocking collectives  121 us (30%)
  starting transfers between devices  31.3 us (8%)
  matrix products  29.6 us (7%)
  local copies, waits for them, and re-layouts  11.8 us (3%)
  other arithmetic  4.39 us (1%)
    all_to_all x2, waiting for transfers between devices, local(): lax.all_to_all(link_terms, ('nx', 'ny'), split_axis=0, concat_axis=0, til...  192 us
    all_to_all x1, blocking collectives, local(): lax.all_to_all(link_terms, ('nx', 'ny'), split_axis=0, concat_axis=0, til...  103 us
    dot_general x3, matrix products, link_products(): jnp.einsum('ier,ers->eis', gathered, masked, preferred_element_type=jnp.f...  18.3 us
    all_to_all x1, blocking collectives, local(): lax.all_to_all(hidden, ('nx', 'ny'), split_axis=0, concat_axis=1, tiled=T...  17.7 us
    all_to_all x2, starting transfers between devices, local(): lax.all_to_all(link_terms, ('nx', 'ny'), split_axis=0, concat_axis=0, til...  16.5 us
    all_to_all x1, starting transfers between devices, local(): lax.all_to_all(features, ('nx', 'ny'), split_axis=1, concat_axis=0, tiled...  14.8 us
    dot_general x3, matrix products, combine_links(): jnp.einsum('dq,dis->iqs', onehot, received, preferred_element_type=jnp.fl...  11.4 us
    all_to_all x1, waiting for transfers between devices, local(): lax.all_to_all(features, ('nx', 'ny'), split_axis=1, concat_axis=0, tiled...  9.63 us
  transfers between devices with their start and end apart: 3, of which 3 were waited for; matrix products, arithmetic and copies ran while one was open for 0% of the time, Pallas kernels for 0%

commit v1 on v0

v1 whole, which is shorter than its diff:
```python
import jax
import jax.numpy as jnp
from jax import lax
from jax.experimental import pallas as pl
from jax.experimental.pallas import tpu as pltpu
from jax.sharding import PartitionSpec as P

MESH = pl.DeviceIdType.MESH
NXC, NZ = 4, 8


def layers_kernel(w_hbm, h0, meta, bias, out, wbuf, act, work, ybuf, r1, r2, zr, metav, colv, metas, cols,
                  wl_sem, ws_sem, wr_sem, ms_sem, mr_sem, cs_sem, cr_sem, loc_sem,
                  ag_s, ag_r, xs_sem, x1_r, x2_r, zs_sem, z_r):
    f32, bf16 = jnp.float32, jnp.bfloat16
    nx, ny, im = lax.axis_index("nx"), lax.axis_index("ny"), lax.axis_index("img")
    x, c = nx // 2, nx % 2
    yl, z = ny // NZ, ny % NZ
    me = yl * 2 + c
    plane = x * NZ + z
    layers = act.shape[0] - 1

    def dev(xx, cc, yy, zz, ii):
        return (xx * 2 + cc, yy * NZ + zz, ii)

    partner = dev(x, 1 - c, yl, z, im)
    near = dev(x, c, 1 - yl, z, im)
    im_up = (im + yl) % 2
    im_dn = (im + 1 - yl) % 2
    xp = dev((x + 1) % NXC, c, yl, z, im)
    xm = dev((x + NXC - 1) % NXC, c, yl, z, im)
    zp = dev(x, c, yl, (z + 1) % NZ, im)
    zm = dev(x, c, yl, (z + NZ - 1) % NZ, im)

    def in_plane(j):
        return dev((x + j // NZ) % NXC, c, yl, (z + j) % NZ, im)

    barrier = pltpu.get_barrier_semaphore()

    def greet(d):
        pl.semaphore_signal(barrier, inc=1, device_id=d, device_id_type=MESH)

    greet(partner)
    for cc in (0, 1):
        greet(dev(x, cc, 1 - yl, z, im_up))
        greet(dev(x, cc, 1 - yl, z, im_dn))

    def greet_plane(j, carry):
        greet(in_plane(j))
        return carry

    lax.fori_loop(1, NXC * NZ, greet_plane, 0)
    pl.semaphore_wait(barrier, 5 + NXC * NZ - 1)

    def remote(src, dst, ss, rs, d):
        return pltpu.make_async_remote_copy(src_ref=src, dst_ref=dst, send_sem=ss, recv_sem=rs,
                                            device_id=d, device_id_type=MESH)

    def w_remote(l, xx, cc, yy, ii, slot):
        first = (xx * 2 + cc) * 2 * NZ + yy * NZ
        return remote(w_hbm.at[l, pl.ds(first, NZ)], wbuf.at[l, me, pl.ds(xx * NZ, NZ)],
                      ws_sem.at[l, slot], wr_sem.at[l, me, xx], dev(x, cc, yy, z, ii))

    def w_copies(l):
        res = []
        for xx in range(NXC):
            res.append(w_remote(l, xx, 1 - c, yl, im, xx))
        for i in range(2):
            for cc in (0, 1):
                res.append(w_remote(l, i, cc, 1 - yl, im_up, 4 + 2 * i + cc))
                res.append(w_remote(l, 2 + i, cc, 1 - yl, im_dn, 8 + 2 * i + cc))
        return res

    def w_local(l, xx):
        first = (xx * 2 + c) * 2 * NZ + yl * NZ
        return pltpu.make_async_copy(w_hbm.at[l, pl.ds(first, NZ)], wbuf.at[l, me, pl.ds(xx * NZ, NZ)],
                                     wl_sem.at[l, xx])

    def start_weights(l):
        for cp in w_copies(l):
            cp.start()
        for xx in range(NXC):
            w_local(l, xx).start()

    def wait_weights(l):
        for xx in range(NXC):
            w_local(l, xx).wait()
        for k in range(1, 4):
            src = (me + k) % 4
            for xx in range(NXC):
                remote(w_hbm.at[l, pl.ds(0, NZ)], wbuf.at[l, src, pl.ds(xx * NZ, NZ)],
                       ws_sem.at[l, 0], wr_sem.at[l, src, xx], partner).wait_recv()

    def ag(l, src, slot, d):
        return remote(act.at[l, src], act.at[l, src], ag_s.at[l, slot], ag_r.at[l, slot], d)

    def gather_start(l):
        ag(l, me, 0, near).start()
        ag(l, me, 1, partner).start()

    nb = (1 - yl) * 2 + c

    def gather_finish(l):
        ag(l, nb, 0, near).wait_recv()
        ag(l, nb, 2, partner).start()
        ag(l, yl * 2 + 1 - c, 1, partner).wait_recv()
        ag(l, (1 - yl) * 2 + 1 - c, 2, partner).wait_recv()
        ag(l, me, 0, near).wait_send()
        ag(l, me, 1, partner).wait_send()
        ag(l, nb, 2, partner).wait_send()

    metav[me] = meta[pl.ds(0, 8), :]
    colv[plane] = meta[pl.ds(8, 8), :]
    act[0, me] = h0[...]

    def meta_cp(k, d):
        return remote(meta.at[pl.ds(0, 8)], metav.at[me], ms_sem.at[k], mr_sem.at[k], d)

    def col_cp(j):
        return remote(meta.at[pl.ds(8, 8)], colv.at[plane], cs_sem.at[j], cr_sem.at[j], in_plane(j))

    meta_cp(0, partner).start()
    meta_cp(1, near).start()
    meta_cp(2, dev(x, 1 - c, 1 - yl, z, im)).start()
    gather_start(0)

    def send_col(j, carry):
        col_cp(j).start()
        return carry

    lax.fori_loop(1, NXC * NZ, send_col, 0)
    start_weights(0)
    gather_finish(0)
    for k, d, src in ((0, partner, yl * 2 + 1 - c), (1, near, nb), (2, dev(x, 1 - c, 1 - yl, z, im), (1 - yl) * 2 + 1 - c)):
        remote(meta.at[pl.ds(0, 8)], metav.at[src], ms_sem.at[k], mr_sem.at[k], d).wait_recv()
        meta_cp(k, d).wait_send()

    def wait_col(j, carry):
        frm = ((x + NXC - j // NZ) % NXC) * NZ + (z + NZ - j % NZ) % NZ
        remote(meta.at[pl.ds(8, 8)], colv.at[frm], cs_sem.at[j], cr_sem.at[j], in_plane(j)).wait_recv()
        col_cp(j).wait_send()
        return carry

    lax.fori_loop(1, NXC * NZ, wait_col, 0)
    cp = pltpu.make_async_copy(metav, metas, loc_sem.at[0])
    cp2 = pltpu.make_async_copy(colv, cols, loc_sem.at[1])
    cp.start()
    cp2.start()
    cp.wait()
    cp2.wait()

    za = [(z + 4 - j) % NZ for j in range(4)]
    zb = [(z + NZ - 3 + j) % NZ for j in range(4)]
    x1, x2, x3 = (x + 1) % NXC, (x + 2) % NXC, (x + 3) % NXC

    def layer(l, carry):
        @pl.when(l > 0)
        def _():
            gather_finish(l)

        @pl.when(l < layers - 1)
        def _():
            start_weights(l + 1)

        wait_weights(l)
        for s in range(4):
            work[s] = act[l, s]

        def one(e, carry):
            dest = ((e // NZ) * 2 + c) * 2 * NZ + yl * NZ + e % NZ
            lhs, rhs = [], []
            for s in range(4):
                src = (x * 2 + s % 2) * 2 * NZ + (s // 2) * NZ + z
                row, live, col = metas[s, l, dest], metas[s, 3 + l, dest], cols[e, l, src]
                lhs.append(work[s, row])
                block = wbuf[l, s, e]
                key = jnp.where(live == 1, col, 4)
                rhs.append(jnp.concatenate(
                    [jnp.where(key == k, block, jnp.zeros_like(block)) for k in range(4)], axis=1))
            res = jnp.dot(jnp.concatenate(lhs, axis=1), jnp.concatenate(rhs, axis=0), preferred_element_type=f32)
            for k in range(4):
                ybuf[e // NZ, e % NZ, k] = res[:, k * 128:(k + 1) * 128].astype(bf16)
            return carry

        lax.fori_loop(0, NXC * NZ, one, 0)

        def s1(side, j):
            zz = za[j] if side == 0 else zb[j]
            return remote(ybuf.at[x2, zz], r1.at[l, side, j], xs_sem.at[l, side, j], x1_r.at[l, side, j],
                          xp if side == 0 else xm)

        def s2(side, p):
            zz = za[p] if p < 4 else zb[p - 4]
            return remote(ybuf.at[x1 if side == 0 else x3, zz], r2.at[l, side, p], xs_sem.at[l, side, 4 + p],
                          x2_r.at[l, side, p], xp if side == 0 else xm)

        for j in range(4):
            s1(0, j).start()
            s1(1, j).start()
        for j in range(4):
            s2(0, 4 + j).start()
            s2(1, j).start()
            for side, p in ((0, j), (1, 4 + j)):
                s1(side, j).wait_recv()
                xx, zz = (x1, za[j]) if side == 0 else (x3, zb[j])
                ybuf[xx, zz] = (ybuf[xx, zz].astype(f32) + r1[l, side, j].astype(f32)).astype(bf16)
                s2(side, p).start()

        def zcp(side, o):
            d, slot = (zp, 4 - o) if side == 0 else (zm, 4 + 3 + o)
            zz = (z + o + NZ) % NZ
            return remote(ybuf.at[x, zz], zr.at[l, slot], zs_sem.at[l, slot], z_r.at[l, slot], d)

        def total(p, zz):
            s2(0, p).wait_recv()
            s2(1, p).wait_recv()
            return (ybuf[x, zz].astype(f32) + r2[l, 0, p].astype(f32)) + r2[l, 1, p].astype(f32)

        for j in range(4):
            acc = total(j, za[j])
            if j > 0:
                zcp(0, 5 - j).wait_recv()
                acc = acc + zr[l, j - 1].astype(f32)
            ybuf[x, za[j]] = acc.astype(bf16)
            zcp(0, 4 - j).start()
            acc = total(4 + j, zb[j])
            if j > 0:
                zcp(1, -4 + j).wait_recv()
                acc = acc + zr[l, 4 + j - 1].astype(f32)
            if j < 3:
                ybuf[x, zb[j]] = acc.astype(bf16)
                zcp(1, -3 + j).start()
        zcp(0, 1).wait_recv()
        pre = acc + zr[l, 3].astype(f32) + bias[l]
        act[l + 1, me] = jnp.maximum(pre, 0.0).astype(bf16)

        @pl.when(l < layers - 1)
        def _():
            gather_start(l + 1)

        for side in (0, 1):
            for j in range(4):
                s1(side, j).wait_send()
            for p in range(8):
                s2(side, p).wait_send()
        for j in range(4):
            zcp(0, 4 - j).wait_send()
            if j < 3:
                zcp(1, -3 + j).wait_send()
        for cp in w_copies(l):
            cp.wait_send()
        return carry

    lax.fori_loop(0, layers, layer, 0)
    out[...] = act[layers, me]


def run_layers(w, h0, meta, bias):
    layers, half = w.shape[0], h0.shape[1]
    bf16, DMA = jnp.bfloat16, pltpu.SemaphoreType.DMA
    piece = (4, half, 128)
    vm = pl.BlockSpec(memory_space=pltpu.VMEM)
    return pl.pallas_call(
        layers_kernel,
        out_shape=jax.ShapeDtypeStruct(piece, bf16),
        in_specs=[pl.BlockSpec(memory_space=pl.ANY), vm, vm, vm],
        out_specs=vm,
        scratch_shapes=[
            pltpu.VMEM((layers, 4, NXC * NZ, 128, 128), bf16),
            pltpu.VMEM((layers + 1, 4) + piece, bf16),
            pltpu.VMEM((4,) + piece, bf16),
            pltpu.VMEM((NXC, NZ) + piece, bf16),
            pltpu.VMEM((layers, 2, 4) + piece, bf16),
            pltpu.VMEM((layers, 2, 8) + piece, bf16),
            pltpu.VMEM((layers, 7) + piece, bf16),
            pltpu.VMEM((4, 8, 128), jnp.int32),
            pltpu.VMEM((NXC * NZ, 8, 128), jnp.int32),
            pltpu.SMEM((4, 8, 128), jnp.int32),
            pltpu.SMEM((NXC * NZ, 8, 128), jnp.int32),
            DMA((layers, 4)), DMA((layers, 12)), DMA((layers, 4, 4)),
            DMA((3,)), DMA((3,)), DMA((NXC * NZ,)), DMA((NXC * NZ,)), DMA((2,)),
            DMA((layers, 3)), DMA((layers, 3)),
            DMA((layers, 2, 12)), DMA((layers, 2, 4)), DMA((layers, 2, 8)),
            DMA((layers, 7)), DMA((layers, 7)),
        ],
        compiler_params=pltpu.CompilerParams(
            collective_id=0, has_side_effects=True, vmem_limit_bytes=56 * 1024 * 1024),
    )(w, h0, meta, bias)


def local(features, link_weight, link_row, link_col, link_live, bias):
    hidden = lax.all_to_all(features, ("nx", "ny"), split_axis=1, concat_axis=0, tiled=True)
    rows = hidden.shape[0]
    h0 = hidden.reshape(rows, 4, 128).transpose(1, 0, 2)
    two = jnp.zeros((2, 128), jnp.int32)
    five = jnp.zeros((5, 128), jnp.int32)
    meta = jnp.concatenate([link_row[:, 0], link_live[:, 0], two, link_col[:, :, 0], five], axis=0)
    res = run_layers(link_weight[:, 0], h0, meta, bias.reshape(bias.shape[0], 4, 1, 128))
    hidden = res.transpose(1, 0, 2).reshape(rows, 512)
    return lax.all_to_all(hidden, ("nx", "ny"), split_axis=0, concat_axis=1, tiled=True)


def solution(mesh):
    placed = (
        P(("nx", "ny", "img"), None),
        P(None, ("nx", "ny"), None, None, None),
        P(None, ("nx", "ny"), None),
        P(None, None, ("nx", "ny")),
        P(None, ("nx", "ny"), None),
        P(None, ("nx", "ny")),
    )
    return jax.shard_map(
        local, mesh=mesh, in_specs=placed, out_specs=P(("nx", "ny", "img"), None), check_vma=False
    )
```

time: 400 us -> 240 us (0.60)
  waiting for transfers between devices: 202 us -> 7.13 us
  Pallas kernels: 0 us -> 186 us
  blocking collectives: 121 us -> 21 us
  matrix products: 29.6 us -> 0 us
  starting transfers between devices: 31.3 us -> 14.8 us
    all_to_all x2 -> x0, waiting for transfers between devices: 192 us -> none  [local(): lax.all_to_all(link_terms, ('nx', 'ny'), split_axis=0, concat_axis=0, til...]
    pallas_call x0 -> x1, Pallas kernels: none -> 186 us  [run_layers(): pl.pallas_call(layers_kernel, out_shape=jax.ShapeDtypeStruct(piece, bf16)...]
    all_to_all x1 -> x0, blocking collectives: 103 us -> none  [local(): lax.all_to_all(link_terms, ('nx', 'ny'), split_axis=0, concat_axis=0, til...]
    dot_general x6 -> x0, matrix products: 29.6 us -> none  [the longest x3 18.3 us: link_products(): jnp.einsum('ier,ers->eis', gathered, masked, preferred_element_type=jnp.f...]
    all_to_all x2 -> x0, starting transfers between devices: 16.5 us -> none  [local(): lax.all_to_all(link_terms, ('nx', 'ny'), split_axis=0, concat_axis=0, til...]
    gather x3 -> x0, local copies, waits for them, and re-layouts: 9.15 us -> none  [link_products(): gathered = jnp.take(blocks, row_ids, axis=1)]
  transfers between devices with their start and end apart: 3 -> 1, of which waited for: 3 -> 1; matrix products, arithmetic and copies ran while one was open for 0% -> 2% of each run, Pallas kernels for 0% -> 0%
where the time goes in v1:
time: 240 us
  Pallas kernels  186 us (78%)
  blocking collectives  21 us (9%)
  starting transfers between devices  14.8 us (6%)
  local copies, waits for them, and re-layouts  8.18 us (3%)
  waiting for transfers between devices  7.13 us (3%)
  other arithmetic  2.95 us (1%)
    pallas_call x1, Pallas kernels, run_layers(): pl.pallas_call(layers_kernel, out_shape=jax.ShapeDtypeStruct(piece, bf16)...  186 us
    all_to_all x1, blocking collectives, local(): lax.all_to_all(hidden, ('nx', 'ny'), split_axis=0, concat_axis=1, tiled=T...  21 us
    all_to_all x1, starting transfers between devices, local(): lax.all_to_all(features, ('nx', 'ny'), split_axis=1, concat_axis=0, tiled...  14.8 us
    all_to_all x1, waiting for transfers between devices, local(): lax.all_to_all(features, ('nx', 'ny'), split_axis=1, concat_axis=0, tiled...  7.13 us
  transfers between devices with their start and end apart: 1, of which 1 were waited for; matrix products, arithmetic and copies ran while one was open for 2% of the time, Pallas kernels for 0%

profile of v1, /device:TPU:1, one launch (start us, length us, event | category | flops | bytes accessed | tf_op | source)
XLA Modules:
  0.0 239.7 jit_solution(9675555465545269356)
XLA Ops:
  0.0 0.6 broadcast
  0.6 2.3 reduce
  2.9 0.7 reshape.23
  3.6 14.8 %all-to-all-start = ((bf16[128,2,256]{2,1,0:T(2,128)(2,1)}), bf16[128,2,256]{2,1,0:T(2,128)(2,1)S(1)}, u32[]{:S(2)}, u32[]{:S(2)}) async-start(bf16[128,2,256]{2,1,0:T(2,128)(2,1)} %reshape.23), calls=%async_computation | async-start | bytes 262144 | tf_op jit(solution)/shard_map/all_to_all | solution.py:292
  18.3 0.7 copy.24
  19.0 1.3 reshape.22.bias
  20.3 0.7 copy_bitcast_fusion.1
  21.0 1.2 concatenate.3.meta
  22.2 7.1 %all-to-all-done = bf16[128,2,256]{2,1,0:T(2,128)(2,1)S(1)} async-done(((bf16[128,2,256]{2,1,0:T(2,128)(2,1)}), bf16[128,2,256]{2,1,0:T(2,128)(2,1)S(1)}, u32[]{:S(2)}, u32[]{:S(2)}) %all-to-all-start) | async-done | bytes 131104 | tf_op jit(solution)/shard_map/all_to_all | solution.py:292
  29.4 0.1 reshape.24
  29.5 0.2 copy.14
  29.7 0.8 copy.15
  30.4 185.6 %shard_map.64 = bf16[4,128,128]{2,1,0:T(8,128)(2,1)} custom-call(bf16[3,128,128,128]{3,2,1,0:T(8,128)(2,1)} %bitcast.16, bf16[4,128,128]{2,1,0:T(8,128)(2,1)} %bitcast.18, s32[16,128]{1,0:T(8,128)} %concatenate.3.meta, f32[3,4,1,128]{3,2,1,0:T(1,128)} %reshape.22.bias), custom_call_target="tpu_custom_call" | custom-call | tf_op jit(solution)/shard_map/pallas_call | solution.py:263
  216.0 1.0 copy.16
  217.1 0.7 reduce.1
  217.7 0.1 copy.25
  217.9 21.0 %all_to_all.29 = bf16[128,2,256]{2,1,0:T(2,128)(2,1)S(1)} all-to-all(bf16[128,2,256]{2,1,0:T(2,128)(2,1)S(1)} %reshape.25), channel_id=1, replica_groups=mesh['nx'=8,'ny'=16,'img'=2] {'nx','ny'}, dimensions={0} | all-to-all | bytes 262144 | tf_op jit(solution)/shard_map/all_to_all | solution.py:300
  238.9 0.8 reshape.26
  (3 shorter events, 0.0 us)
Async XLA Ops:
  3.6 25.8 %all-to-all-start = ((bf16[128,2,256]{2,1,0:T(2,128)(2,1)}), bf16[128,2,256]{2,1,0:T(2,128)(2,1)S(1)}, u32[]{:S(2)}, u32[]{:S(2)}) async-start(bf16[128,2,256]{2,1,0:T(2,128)(2,1)} %reshape.23), calls=%async_computation | async-start | bytes 262144 | tf_op jit(solution)/shard_map/all_to_all | solution.py:292

commit v2 on v1

--- a/solution.py
+++ b/solution.py
@@ -9,9 +9,9 @@
 NXC, NZ = 4, 8
 
 
-def layers_kernel(w_hbm, h0, meta, bias, out, wbuf, act, work, ybuf, r1, r2, zr, metav, colv, metas, cols,
+def layers_kernel(w_hbm, feat, meta, bias, out, inb, outb, wbuf, act, work, ybuf, r1, r2, zr, metav, colv, metas, cols,
                   wl_sem, ws_sem, wr_sem, ms_sem, mr_sem, cs_sem, cr_sem, loc_sem,
-                  ag_s, ag_r, xs_sem, x1_r, x2_r, zs_sem, z_r):
+                  in_s, in_r, out_s, out_r, ag_s, ag_r, xs_sem, x1_r, x2_r, zs_sem, z_r):
     f32, bf16 = jnp.float32, jnp.bfloat16
     nx, ny, im = lax.axis_index("nx"), lax.axis_index("ny"), lax.axis_index("img")
     x, c = nx // 2, nx % 2
@@ -40,17 +40,21 @@
     def greet(d):
         pl.semaphore_signal(barrier, inc=1, device_id=d, device_id_type=MESH)
 
-    greet(partner)
+    flat = nx * (2 * NZ) + ny
+    half = 4 * NXC * NZ
+
+    def member(j):
+        k = (flat + j) % half
+        return k, (k // (2 * NZ), k % (2 * NZ), im)
+
+    def greet_half(j, carry):
+        greet(member(j)[1])
+        return carry
+
     for cc in (0, 1):
-        greet(dev(x, cc, 1 - yl, z, im_up))
-        greet(dev(x, cc, 1 - yl, z, im_dn))
-
-    def greet_plane(j, carry):
-        greet(in_plane(j))
-        return carry
-
-    lax.fori_loop(1, NXC * NZ, greet_plane, 0)
-    pl.semaphore_wait(barrier, 5 + NXC * NZ - 1)
+        greet(dev(x, cc, 1 - yl, z, 1 - im))
+    lax.fori_loop(1, half, greet_half, 0)
+    pl.semaphore_wait(barrier, 2 + half - 1)
 
     def remote(src, dst, ss, rs, d):
         return pltpu.make_async_remote_copy(src_ref=src, dst_ref=dst, send_sem=ss, recv_sem=rs,
@@ -61,14 +65,12 @@
         return remote(w_hbm.at[l, pl.ds(first, NZ)], wbuf.at[l, me, pl.ds(xx * NZ, NZ)],
                       ws_sem.at[l, slot], wr_sem.at[l, me, xx], dev(x, cc, yy, z, ii))
 
-    def w_copies(l):
-        res = []
-        for xx in range(NXC):
-            res.append(w_remote(l, xx, 1 - c, yl, im, xx))
-        for i in range(2):
-            for cc in (0, 1):
-                res.append(w_remote(l, i, cc, 1 - yl, im_up, 4 + 2 * i + cc))
-                res.append(w_remote(l, 2 + i, cc, 1 - yl, im_dn, 8 + 2 * i + cc))
+    def w_copies(l, part):
+        i = part
+        res = [w_remote(l, 2 * i, 1 - c, yl, im, 2 * i), w_remote(l, 2 * i + 1, 1 - c, yl, im, 2 * i + 1)]
+        for cc in (0, 1):
+            res.append(w_remote(l, i, cc, 1 - yl, im_up, 4 + 2 * i + cc))
+            res.append(w_remote(l, 2 + i, cc, 1 - yl, im_dn, 8 + 2 * i + cc))
         return res
 
     def w_local(l, xx):
@@ -76,11 +78,12 @@
         return pltpu.make_async_copy(w_hbm.at[l, pl.ds(first, NZ)], wbuf.at[l, me, pl.ds(xx * NZ, NZ)],
                                      wl_sem.at[l, xx])
 
-    def start_weights(l):
-        for cp in w_copies(l):
+    def start_weights(l, part):
+        for cp in w_copies(l, part):
             cp.start()
-        for xx in range(NXC):
-            w_local(l, xx).start()
+        if part == 0:
+            for xx in range(NXC):
+                w_local(l, xx).start()
 
     def wait_weights(l):
         for xx in range(NXC):
@@ -109,9 +112,19 @@
         ag(l, me, 1, partner).wait_send()
         ag(l, nb, 2, partner).wait_send()
 
+    def in_cp(j):
+        k, d = member(j)
+        return remote(feat.at[k], inb.at[flat], in_s, in_r, d)
+
+    def send_in(j, carry):
+        in_cp(j).start()
+        return carry
+
+    lax.fori_loop(1, half, send_in, 0)
+    inb[flat] = feat[flat]
+
     metav[me] = meta[pl.ds(0, 8), :]
     colv[plane] = meta[pl.ds(8, 8), :]
-    act[0, me] = h0[...]
 
     def meta_cp(k, d):
         return remote(meta.at[pl.ds(0, 8)], metav.at[me], ms_sem.at[k], mr_sem.at[k], d)
@@ -122,15 +135,21 @@
     meta_cp(0, partner).start()
     meta_cp(1, near).start()
     meta_cp(2, dev(x, 1 - c, 1 - yl, z, im)).start()
-    gather_start(0)
 
     def send_col(j, carry):
         col_cp(j).start()
         return carry
 
     lax.fori_loop(1, NXC * NZ, send_col, 0)
-    start_weights(0)
+    start_weights(0, 0)
+    lot = remote(feat.at[pl.ds(0, half - 1)], inb.at[pl.ds(0, half - 1)], in_s, in_r, partner)
+    lot.wait_recv()
+    for r in range(4):
+        act[0, me, r] = inb[:, r, 0, :].astype(f32).astype(bf16)
+    gather_start(0)
+    start_weights(0, 1)
     gather_finish(0)
+    lot.wait_send()
     for k, d, src in ((0, partner, yl * 2 + 1 - c), (1, near, nb), (2, dev(x, 1 - c, 1 - yl, z, im), (1 - yl) * 2 + 1 - c)):
         remote(meta.at[pl.ds(0, 8)], metav.at[src], ms_sem.at[k], mr_sem.at[k], d).wait_recv()
         meta_cp(k, d).wait_send()
@@ -160,7 +179,8 @@
 
         @pl.when(l < layers - 1)
         def _():
-            start_weights(l + 1)
+            start_weights(l + 1, 0)
+            start_weights(l + 1, 1)
 
         wait_weights(l)
         for s in range(4):
@@ -247,25 +267,39 @@
             zcp(0, 4 - j).wait_send()
             if j < 3:
                 zcp(1, -3 + j).wait_send()
-        for cp in w_copies(l):
+        for cp in w_copies(l, 0) + w_copies(l, 1):
             cp.wait_send()
         return carry
 
     lax.fori_loop(0, layers, layer, 0)
-    out[...] = act[layers, me]
-
-
-def run_layers(w, h0, meta, bias):
-    layers, half = w.shape[0], h0.shape[1]
+    for r in range(4):
+        outb[:, r, 0, :] = act[layers, me, r]
+
+    def send_out(j, carry):
+        k, d = member(j)
+        remote(outb.at[k], out.at[flat], out_s, out_r, d).start()
+        return carry
+
+    lax.fori_loop(1, half, send_out, 0)
+    out[flat] = outb[flat]
+    lot = remote(outb.at[pl.ds(0, half - 1)], out.at[pl.ds(0, half - 1)], out_s, out_r, partner)
+    lot.wait_recv()
+    lot.wait_send()
+
+
+def run_layers(w, feat, meta, bias):
+    layers, half = w.shape[0], feat.shape[0]
     bf16, DMA = jnp.bfloat16, pltpu.SemaphoreType.DMA
     piece = (4, half, 128)
     vm = pl.BlockSpec(memory_space=pltpu.VMEM)
     return pl.pallas_call(
         layers_kernel,
-        out_shape=jax.ShapeDtypeStruct(piece, bf16),
+        out_shape=jax.ShapeDtypeStruct(feat.shape, bf16),
         in_specs=[pl.BlockSpec(memory_space=pl.ANY), vm, vm, vm],
         out_specs=vm,
         scratch_shapes=[
+            pltpu.VMEM(feat.shape, bf16),
+            pltpu.VMEM(feat.shape, bf16),
             pltpu.VMEM((layers, 4, NXC * NZ, 128, 128), bf16),
             pltpu.VMEM((layers + 1, 4) + piece, bf16),
             pltpu.VMEM((4,) + piece, bf16),
@@ -279,25 +313,23 @@
             pltpu.SMEM((NXC * NZ, 8, 128), jnp.int32),
             DMA((layers, 4)), DMA((layers, 12)), DMA((layers, 4, 4)),
             DMA((3,)), DMA((3,)), DMA((NXC * NZ,)), DMA((NXC * NZ,)), DMA((2,)),
+            DMA, DMA, DMA, DMA,
             DMA((layers, 3)), DMA((layers, 3)),
             DMA((layers, 2, 12)), DMA((layers, 2, 4)), DMA((layers, 2, 8)),
             DMA((layers, 7)), DMA((layers, 7)),
         ],
         compiler_params=pltpu.CompilerParams(
             collective_id=0, has_side_effects=True, vmem_limit_bytes=56 * 1024 * 1024),
-    )(w, h0, meta, bias)
+    )(w, feat, meta, bias)
 
 
 def local(features, link_weight, link_row, link_col, link_live, bias):
-    hidden = lax.all_to_all(features, ("nx", "ny"), split_axis=1, concat_axis=0, tiled=True)
-    rows = hidden.shape[0]
-    h0 = hidden.reshape(rows, 4, 128).transpose(1, 0, 2)
     two = jnp.zeros((2, 128), jnp.int32)
     five = jnp.zeros((5, 128), jnp.int32)
     meta = jnp.concatenate([link_row[:, 0], link_live[:, 0], two, link_col[:, :, 0], five], axis=0)
-    res = run_layers(link_weight[:, 0], h0, meta, bias.reshape(bias.shape[0], 4, 1, 128))
-    hidden = res.transpose(1, 0, 2).reshape(rows, 512)
-    return lax.all_to_all(hidden, ("nx", "ny"), split_axis=0, concat_axis=1, tiled=True)
+    res = run_layers(link_weight[:, 0], features.reshape(128, 4, 1, 128), meta,
+                     bias.reshape(bias.shape[0], 4, 1, 128))
+    return res.reshape(features.shape)
 
 
 def solution(mesh):

time: 240 us -> 216 us (0.900)
  Pallas kernels: 186 us -> 210 us
  blocking collectives: 21 us -> 0 us
  starting transfers between devices: 14.8 us -> 0 us
  waiting for transfers between devices: 7.13 us -> 0 us
  other arithmetic: 2.95 us -> 0 us
    pallas_call x1, Pallas kernels: 186 us -> 210 us  [run_layers(): pl.pallas_call(layers_kernel, out_shape=jax.ShapeDtypeStruct(feat.shape,...]
    all_to_all x1 -> x0, blocking collectives: 21 us -> none  [local(): lax.all_to_all(hidden, ('nx', 'ny'), split_axis=0, concat_axis=1, tiled=T...]
    all_to_all x1 -> x0, starting transfers between devices: 14.8 us -> none  [local(): lax.all_to_all(features, ('nx', 'ny'), split_axis=1, concat_axis=0, tiled...]
    all_to_all x1 -> x0, waiting for transfers between devices: 7.13 us -> none  [local(): lax.all_to_all(features, ('nx', 'ny'), split_axis=1, concat_axis=0, tiled...]
  transfers between devices with their start and end apart: 1 -> 0, of which waited for: 1 -> 0; matrix products, arithmetic and copies ran while one was open for 2% -> 0% of each run, Pallas kernels for 0% -> 0%
where the time goes in v2:
time: 216 us; the launch traced here: 215 us
  Pallas kernels  210 us (97%)
  local copies, waits for them, and re-layouts  5.82 us (3%)
    pallas_call x1, Pallas kernels, run_layers(): pl.pallas_call(layers_kernel, out_shape=jax.ShapeDtypeStruct(feat.shape,...  210 us

profile of v2, /device:TPU:1, one launch (start us, length us, event | category | flops | bytes accessed | tf_op | source)
XLA Modules:
  0.0 215.4 jit_solution(17127108235276791706)
XLA Ops:
  0.0 0.7 copy.13
  0.7 0.7 copy_bitcast_fusion.1
  1.4 1.2 concatenate.3.meta
  2.6 1.3 reshape.10.bias
  3.9 209.6 %shard_map.64 = bf16[128,4,1,128]{3,2,1,0:T(2,128)(2,1)} custom-call(bf16[3,128,128,128]{3,2,1,0:T(8,128)(2,1)} %bitcast.10, bf16[128,4,1,128]{3,2,1,0:T(2,128)(2,1)} %bitcast.12, s32[16,128]{1,0:T(8,128)} %concatenate.3.meta, f32[3,4,1,128]{3,2,1,0:T(1,128)} %reshape.10.bias), custom_call_target="tpu_custom_call" | custom-call | tf_op jit(solution)/shard_map/pallas_call | solution.py:295
  213.5 1.9 copy.15
  (2 shorter events, 0.0 us)

commit v3 on v0

v3 whole, which is shorter than its diff:
```python
import jax
import jax.numpy as jnp
from jax import lax
from jax.experimental import pallas as pl
from jax.experimental.pallas import tpu as pltpu
from jax.sharding import PartitionSpec as P

MESH = pl.DeviceIdType.MESH
NXC, NZ = 4, 8
NY = 2 * NZ
HALF = 2 * NXC * NY
HA = 64
HB = HALF - HA
UP = (0, 1, 3, 5)
DOWN = (0, 2, 4, 6)


def bslot(side, level, role):
    return side * 2 + role % 2 if level == 0 else 4 + ((level - 1) * 2 + side) * 4 + role


def layers_kernel(w_hbm, feat, meta, bias, out, inb, outb, wbuf, acta, actb, work,
                  yab, yaf, sa, saz, ybf, sbz, sbx, ra, zra, zrb, rb, metav, colv, metas, cols,
                  wl_sem, ws_sem, wr_sem, ms_sem, mr_sem, cs_sem, cr_sem, loc_sem,
                  in_s, in_r, out_s, out_r, ag_s, ag_r,
                  sa_sem, ra_sem, sza_sem, rza_sem, szb_sem, rzb_sem, sxb_sem, rxb_sem):
    f32, bf16 = jnp.float32, jnp.bfloat16
    nx, ny, im = lax.axis_index("nx"), lax.axis_index("ny"), lax.axis_index("img")
    x, c = nx // 2, nx % 2
    yl, z = ny // NZ, ny % NZ
    me = yl * 2 + c
    plane = x * NZ + z
    flat = nx * NY + ny
    layers = wbuf.shape[0]

    def dev(xx, cc, yy, zz, ii):
        return (xx * 2 + cc, yy * NZ + zz, ii)

    partner = dev(x, 1 - c, yl, z, im)
    near = dev(x, c, 1 - yl, z, im)
    diag = dev(x, 1 - c, 1 - yl, z, im)
    im_up = (im + yl) % 2
    im_dn = (im + 1 - yl) % 2
    x1, x2, x3 = (x + 1) % NXC, (x + 2) % NXC, (x + 3) % NXC
    xp, xm = dev(x1, c, yl, z, im), dev(x3, c, yl, z, im)
    zp = dev(x, c, yl, (z + 1) % NZ, im)
    zm = dev(x, c, yl, (z + NZ - 1) % NZ, im)

    def col_z(k):
        far = 4 - (k + 1) // 2
        return (z + NZ + jnp.where(k % 2 == 1, far, -far)) % NZ

    def for_half(fn):
        for b in range(1, NY):
            fn(nx * NY + (ny + b) % NY, (nx, (ny + b) % NY, im))

        def rows(a, carry):
            n = (nx + a) % (2 * NXC)
            for b in range(NY):
                fn(n * NY + (ny + b) % NY, (n, (ny + b) % NY, im))
            return carry

        lax.fori_loop(1, 2 * NXC, rows, 0)

    def for_plane(fn):
        def step(j, carry):
            fn(j, dev((x + j // NZ) % NXC, c, yl, (z + j) % NZ, im))
            return carry

        lax.fori_loop(1, NXC * NZ, step, 0)

    def remote(src, dst, ss, rs, d):
        return pltpu.make_async_remote_copy(src_ref=src, dst_ref=dst, send_sem=ss, recv_sem=rs,
                                            device_id=d, device_id_type=MESH)

    barrier = pltpu.get_barrier_semaphore()

    def greet(k, d):
        pl.semaphore_signal(barrier, inc=1, device_id=d, device_id_type=MESH)

    for cc in (0, 1):
        greet(0, dev(x, cc, 1 - yl, z, 1 - im))
    for_half(greet)
    pl.semaphore_wait(barrier, 2 + HALF - 1)

    for_half(lambda k, d: remote(feat.at[k], inb.at[flat], in_s, in_r, d).start())

    metav[me] = meta[pl.ds(0, 8), :]
    colv[plane] = meta[pl.ds(8, 8), :]

    def meta_cp(k, d):
        return remote(meta.at[pl.ds(0, 8)], metav.at[me], ms_sem.at[k], mr_sem.at[k], d)

    group = ((0, partner, yl * 2 + 1 - c), (1, near, (1 - yl) * 2 + c), (2, diag, (1 - yl) * 2 + 1 - c))
    for k, d, _ in group:
        meta_cp(k, d).start()
    for_plane(lambda j, d: remote(meta.at[pl.ds(8, 8)], colv.at[plane], cs_sem, cr_sem, d).start())

    def start_weights(l, lo, hi):
        def step(k, carry):
            zz = col_z(k)

            def send(x0, n, cc, yy, ii):
                remote(w_hbm.at[l, pl.ds(x0, n), cc, yy, zz], wbuf.at[l, me, k, pl.ds(x0, n)],
                       ws_sem.at[l], wr_sem.at[l, k], dev(x, cc, yy, z, ii)).start()

            for cc in (0, 1):
                send(0, 2, cc, 1 - yl, im_up)
                send(2, 2, cc, 1 - yl, im_dn)
            send(0, 4, 1 - c, yl, im)
            pltpu.make_async_copy(w_hbm.at[l, :, c, yl, zz], wbuf.at[l, me, k], wl_sem.at[l, k]).start()
            return carry

        lax.fori_loop(lo, hi, step, 0)

    def wait_weights(l, k):
        pltpu.make_async_copy(w_hbm.at[l, :, c, yl, 0], wbuf.at[l, me, k], wl_sem.at[l, k]).wait()
        three = wbuf.at[l, pl.ds(0, 3), k]
        remote(three, three, ws_sem.at[l], wr_sem.at[l, k], partner).wait_recv()

    acts = (acta, actb)

    def ag(l, st, src, slot, d):
        ref = acts[st].at[l, src]
        return remote(ref, ref, ag_s.at[l, st, slot], ag_r.at[l, st, slot], d)

    def gather_start(l, st):
        ag(l, st, me, 0, near).start()
        ag(l, st, me, 1, partner).start()

    def gather_finish(l):
        for st in (0, 1):
            ag(l, st, (1 - yl) * 2 + c, 0, near).wait_recv()
            ag(l, st, (1 - yl) * 2 + c, 2, partner).start()
        for st in (0, 1):
            ag(l, st, yl * 2 + 1 - c, 1, partner).wait_recv()
            ag(l, st, (1 - yl) * 2 + 1 - c, 2, partner).wait_recv()

    def gather_sent(l):
        for st in (0, 1):
            ag(l, st, me, 0, near).wait_send()
            ag(l, st, me, 1, partner).wait_send()
            ag(l, st, me, 2, partner).wait_send()

    start_weights(0, 0, 2)
    for k, d, src in group:
        remote(meta.at[pl.ds(0, 8)], metav.at[src], ms_sem.at[k], mr_sem.at[k], d).wait_recv()
        meta_cp(k, d).wait_send()
    lot = remote(colv.at[pl.ds(0, NXC * NZ - 1)], colv.at[pl.ds(0, NXC * NZ - 1)], cs_sem, cr_sem, partner)
    lot.wait_recv()
    lot.wait_send()
    tables = (pltpu.make_async_copy(metav, metas, loc_sem.at[0]), pltpu.make_async_copy(colv, cols, loc_sem.at[1]))
    for cp in tables:
        cp.start()
    inb[flat] = feat[flat]
    lot = remote(feat.at[pl.ds(0, HALF - 1)], inb.at[pl.ds(0, HALF - 1)], in_s, in_r, partner)
    lot.wait_recv()
    for r in range(4):
        rows = inb[:, r, 0, :].astype(f32).astype(bf16)
        acta[0, me, r] = rows[:HA]
        actb[0, me, r] = rows[HA:]
    gather_start(0, 0)
    gather_start(0, 1)
    lot.wait_send()
    for cp in tables:
        cp.wait()

    def layer(l, carry):
        @pl.when(l == 0)
        def _():
            start_weights(l, 2, 8)

        @pl.when(l > 0)
        def _():
            start_weights(l, 6, 8)

        gather_finish(l)

        @pl.when(l < layers - 1)
        def _():
            start_weights(l + 1, 0, 6)

        for s in range(4):
            work[s, :, pl.ds(0, HA)] = acta[l, s]
            work[s, :, pl.ds(HA, HB)] = actb[l, s]

        def xa(k, kind, src, d):
            return remote(src, ra.at[l, kind, k], sa_sem.at[l], ra_sem.at[l, kind, k], d)

        def zb(side, level, role):
            n = bslot(side, level, role)
            return remote(sbz.at[n], zrb.at[l, n], szb_sem.at[l], rzb_sem.at[l, n], zm if side else zp)

        def zb_now(side, level, k, role):
            sbz[bslot(side, level, role)] = ybf[k, role].astype(bf16)
            zb(side, level, role).start()

        def column(k, carry):
            wait_weights(l, k)
            zz = col_z(k)
            towards = jnp.logical_or(k % 2 == 1, k == 0)
            pick = jnp.where(towards, 1, 0)
            xs = (x2, jnp.where(towards, x1, x3), jnp.where(towards, x3, x1), x)
            roles = (0, 2 - pick, 1 + pick, 3)
            for n in range(4):
                dest = (xs[n] * 2 + c) * NY + yl * NZ + zz
                lhs, rhs = [], []
                for s in range(4):
                    src = (x * 2 + s % 2) * NY + (s // 2) * NZ + z
                    row, live, col = metas[s, l, dest], metas[s, 3 + l, dest], cols[xs[n] * NZ + zz, l, src]
                    lhs.append(work[s, row])
                    block = wbuf[l, s, k, xs[n]]
                    key = jnp.where(live == 1, col, 4)
                    rhs.append(jnp.concatenate(
                        [jnp.where(key == q, block, jnp.zeros_like(block)) for q in range(4)], axis=1))
                res = jnp.dot(jnp.concatenate(lhs, axis=1), jnp.concatenate(rhs, axis=0), preferred_element_type=f32)
                for q in range(4):
                    part = res[:, q * 128:(q + 1) * 128]
                    ybf[k, roles[n], q] = part[HA:]
                    if n == 0:
                        yab[k, 0, q] = part[:HA].astype(bf16)
                    elif n == 2:
                        yab[k, 1, q] = part[:HA].astype(bf16)
                    else:
                        yaf[k, n // 2, q] = part[:HA]
            first = tuple(jnp.where(towards, p, m) for p, m in zip(xp, xm))
            xa(k, 0, yab.at[k, 0], first).start()

            @pl.when(k == 0)
            def _():
                for role in range(4):
                    zb_now(role // 2, 0, 0, role)

            @pl.when(k == 1)
            def _():
                for role in (2, 3):
                    zb_now(0, 1, 1, role)

            @pl.when(k == 2)
            def _():
                for role in (0, 1):
                    zb_now(1, 1, 2, role)

            @pl.when(k % 2 == 0)
            def _():
                @pl.when(k < 3)
                def _():
                    other = tuple(jnp.where(towards, m, p) for p, m in zip(xp, xm))
                    xa(k, 1, yab.at[k, 1], other).start()

            return carry

        lax.fori_loop(0, NZ, column, 0)

        def a_plus(k):
            return k % 2 == 1 or k == 0

        def a_imm(k):
            xa(k, 1, yab.at[k, 1], xm if a_plus(k) else xp).start()

        def a_acc(k):
            xa(k, 0, yab.at[k, 0], xp).wait_recv()
            sa[k] = (yaf[k, 0] + ra[l, 0, k].astype(f32)).astype(bf16)
            xa(k, 2, sa.at[k], xp if a_plus(k) else xm).start()

        def za(k):
            return remote(saz.at[k], zra.at[l, k], sza_sem.at[l], rza_sem.at[l, k], zp if a_plus(k) else zm)

        def a_total(k):
            for kind in (1, 2):
                xa(k, kind, sa.at[k], xp).wait_recv()
            acc = (yaf[k, 1] + ra[l, 1, k].astype(f32)) + ra[l, 2, k].astype(f32)
            for chain in (UP, DOWN[1:]):
                seq = chain + (7,)
                for p in range(1, len(seq)):
                    if seq[p] == k:
                        za(seq[p - 1]).wait_recv()
                        acc = acc + zra[l, seq[p - 1]].astype(f32)
            if k < 7:
                saz[k] = acc.astype(bf16)
                za(k).start()
            else:
                acta[l + 1, me] = jnp.maximum(acc + bias[l], 0.0).astype(bf16)

        def b_step(level, role):
            for side, chain in ((0, UP), (1, DOWN)):
                if level == 1 and role // 2 != side:
                    continue
                zb(side, level - 1, role).wait_recv()
                n = bslot(side, level, role)
                sbz[n] = (ybf[chain[level], role] + zrb[l, bslot(side, level - 1, role)].astype(f32)).astype(bf16)
                zb(side, level, role).start()

        def xb(n, d):
            return remote(sbx.at[n], rb.at[l, n], sxb_sem.at[l], rxb_sem.at[l, n], d)

        def b_sum(role):
            for side in (0, 1):
                zb(side, 3, role).wait_recv()
            return ybf[7, role] + zrb[l, bslot(0, 3, role)].astype(f32) + zrb[l, bslot(1, 3, role)].astype(f32)

        def b_far():
            acc = b_sum(0)
            sbx[0] = acc[0:2].astype(bf16)
            xb(0, xp).start()
            sbx[1] = acc[2:4].astype(bf16)
            xb(1, xm).start()

        def b_next(side):
            acc = b_sum(1 + side)
            lo, hi = (0, 2) if side == 0 else (2, 0)
            d = xm if side else xp
            sbx[3 + 2 * side] = acc[hi:hi + 2].astype(bf16)
            xb(3 + 2 * side, d).start()
            xb(side, d).wait_recv()
            sbx[2 + 2 * side] = (acc[lo:lo + 2] + rb[l, side].astype(f32)).astype(bf16)
            xb(2 + 2 * side, d).start()

        def b_final():
            ybf[7, 3] = b_sum(3)
            for n in range(2, 6):
                xb(n, xp).wait_recv()
            for lo, up, dn in ((0, 2, 5), (2, 3, 4)):
                acc = ybf[7, 3, lo:lo + 2] + rb[l, up].astype(f32) + rb[l, dn].astype(f32)
                actb[l + 1, me, lo:lo + 2] = jnp.maximum(acc + bias[l, lo:lo + 2], 0.0).astype(bf16)

        a_acc(0)
        a_acc(2)
        for role in (0, 2, 1, 3):
            b_step(1, role)
        for k in (1, 4, 3):
            a_imm(k)
            a_acc(k)
        a_imm(6)
        b_step(2, 0)
        a_acc(6)
        a_imm(5)
        a_acc(5)
        b_step(2, 1)
        a_imm(7)
        a_acc(7)
        b_step(2, 2)
        a_total(0)
        b_step(2, 3)
        a_total(1)
        a_total(2)
        b_step(3, 0)
        b_step(3, 1)
        a_total(3)
        b_step(3, 2)
        a_total(4)
        b_step(3, 3)
        b_far()
        a_total(5)
        b_next(0)
        b_next(1)
        a_total(6)
        a_total(7)

        @pl.when(l < layers - 1)
        def _():
            gather_start(l + 1, 0)

        b_final()

        @pl.when(l < layers - 1)
        def _():
            gather_start(l + 1, 1)

        gather_sent(l)
        for ref, sem in ((ra, sa_sem), (zra, sza_sem), (zrb, szb_sem), (rb, sxb_sem)):
            remote(ref.at[l], ref.at[l], sem.at[l], ra_sem.at[l, 0, 0], partner).wait_send()
        sent = wbuf.at[l, pl.ds(0, 3)]
        remote(sent, sent, ws_sem.at[l], wr_sem.at[l, 0], partner).wait_send()
        return carry

    lax.fori_loop(0, layers, layer, 0)

    for r in range(4):
        outb[pl.ds(0, HA), r, 0, :] = acta[layers, me, r]
        outb[pl.ds(HA, HB), r, 0, :] = actb[layers, me, r]
    for_half(lambda k, d: remote(outb.at[k], out.at[flat], out_s, out_r, d).start())
    out[flat] = outb[flat]
    lot = remote(outb.at[pl.ds(0, HALF - 1)], out.at[pl.ds(0, HALF - 1)], out_s, out_r, partner)
    lot.wait_recv()
    lot.wait_send()


def run_layers(w, feat, meta, bias):
    layers = w.shape[0]
    bf16, f32, DMA = jnp.bfloat16, jnp.float32, pltpu.SemaphoreType.DMA
    pa, pb, hb = (4, HA, 128), (4, HB, 128), (2, HB, 128)
    vm = pl.BlockSpec(memory_space=pltpu.VMEM)
    return pl.pallas_call(
        layers_kernel,
        out_shape=jax.ShapeDtypeStruct(feat.shape, bf16),
        in_specs=[pl.BlockSpec(memory_space=pl.ANY), vm, vm, vm],
        out_specs=vm,
        scratch_shapes=[
            pltpu.VMEM(feat.shape, bf16),
            pltpu.VMEM(feat.shape, bf16),
            pltpu.VMEM((layers, 4, NZ, NXC, 128, 128), bf16),
            pltpu.VMEM((layers + 1, 4) + pa, bf16),
            pltpu.VMEM((layers + 1, 4) + pb, bf16),
            pltpu.VMEM((4, 4, HALF, 128), bf16),
            pltpu.VMEM((NZ, 2) + pa, bf16),
            pltpu.VMEM((NZ, 2) + pa, f32),
            pltpu.VMEM((NZ,) + pa, bf16),
            pltpu.VMEM((NZ - 1,) + pa, bf16),
            pltpu.VMEM((NZ, 4) + pb, f32),
            pltpu.VMEM((28,) + pb, bf16),
            pltpu.VMEM((6,) + hb, bf16),
            pltpu.VMEM((layers, 3, NZ) + pa, bf16),
            pltpu.VMEM((layers, NZ - 1) + pa, bf16),
            pltpu.VMEM((layers, 28) + pb, bf16),
            pltpu.VMEM((layers, 6) + hb, bf16),
            pltpu.VMEM((4, 8, 128), jnp.int32),
            pltpu.VMEM((NXC * NZ, 8, 128), jnp.int32),
            pltpu.SMEM((4, 8, 128), jnp.int32),
            pltpu.SMEM((NXC * NZ, 8, 128), jnp.int32),
            DMA((layers, NZ)), DMA((layers,)), DMA((layers, NZ)),
            DMA((3,)), DMA((3,)), DMA, DMA, DMA((2,)),
            DMA, DMA, DMA, DMA,
            DMA((layers, 2, 3)), DMA((layers, 2, 3)),
            DMA((layers,)), DMA((layers, 3, NZ)),
            DMA((layers,)), DMA((layers, NZ - 1)),
            DMA((layers,)), DMA((layers, 28)),
            DMA((layers,)), DMA((layers, 6)),
        ],
        compiler_params=pltpu.CompilerParams(
            collective_id=0, has_side_effects=True, vmem_limit_bytes=60 * 1024 * 1024),
    )(w, feat, meta, bias)


def local(features, link_weight, link_row, link_col, link_live, bias):
    two = jnp.zeros((2, 128), jnp.int32)
    five = jnp.zeros((5, 128), jnp.int32)
    meta = jnp.concatenate([link_row[:, 0], link_live[:, 0], two, link_col[:, :, 0], five], axis=0)
    layers = bias.shape[0]
    res = run_layers(link_weight.reshape(layers, NXC, 2, 2, NZ, 128, 128), features.reshape(HALF, 4, 1, 128), meta,
                     bias.reshape(layers, 4, 1, 128))
    return res.reshape(features.shape)


def solution(mesh):
    placed = (
        P(("nx", "ny", "img"), None),
        P(None, ("nx", "ny"), None, None, None),
        P(None, ("nx", "ny"), None),
        P(None, None, ("nx", "ny")),
        P(None, ("nx", "ny"), None),
        P(None, ("nx", "ny")),
    )
    return jax.shard_map(
        local, mesh=mesh, in_specs=placed, out_specs=P(("nx", "ny", "img"), None), check_vma=False
    )
```

time: 400 us -> 166 us (0.41)
  waiting for transfers between devices: 202 us -> 0 us
  Pallas kernels: 0 us -> 160 us
  blocking collectives: 121 us -> 0 us
  starting transfers between devices: 31.3 us -> 0 us
  matrix products: 29.6 us -> 0 us
  local copies, waits for them, and re-layouts: 11.8 us -> 5.82 us
  other arithmetic: 4.39 us -> 0 us
    all_to_all x3 -> x0, waiting for transfers between devices: 202 us -> none  [the longest x2 192 us: local(): lax.all_to_all(link_terms, ('nx', 'ny'), split_axis=0, concat_axis=0, til...]
    pallas_call x0 -> x1, Pallas kernels: none -> 160 us  [run_layers(): pl.pallas_call(layers_kernel, out_shape=jax.ShapeDtypeStruct(feat.shape,...]
    all_to_all x2 -> x0, blocking collectives: 121 us -> none  [the longest x1 103 us: local(): lax.all_to_all(link_terms, ('nx', 'ny'), split_axis=0, concat_axis=0, til...]
    all_to_all x3 -> x0, starting transfers between devices: 31.3 us -> none  [the longest x2 16.5 us: local(): lax.all_to_all(link_terms, ('nx', 'ny'), split_axis=0, concat_axis=0, til...]
    dot_general x6 -> x0, matrix products: 29.6 us -> none  [the longest x3 18.3 us: link_products(): jnp.einsum('ier,ers->eis', gathered, masked, preferred_element_type=jnp.f...]
    gather x3 -> x0, local copies, waits for them, and re-layouts: 9.15 us -> none  [link_products(): gathered = jnp.take(blocks, row_ids, axis=1)]
  transfers between devices with their start and end apart: 3 -> 0, of which waited for: 3 -> 0; matrix products, arithmetic and copies ran while one was open for 0% -> 0% of each run, Pallas kernels for 0% -> 0%
where the time goes in v3:
time: 166 us
  Pallas kernels  160 us (96%)
  local copies, waits for them, and re-layouts  5.82 us (4%)
    pallas_call x1, Pallas kernels, run_layers(): pl.pallas_call(layers_kernel, out_shape=jax.ShapeDtypeStruct(feat.shape,...  160 us

profile of v3, /device:TPU:1, one launch (start us, length us, event | category | flops | bytes accessed | tf_op | source)
XLA Modules:
  0.0 166.1 jit_solution(6126019196511706073)
XLA Ops:
  0.0 0.7 copy.13
  0.7 0.7 copy_bitcast_fusion.1
  1.4 1.2 concatenate.3.meta
  2.6 1.3 reshape.14.bias
  3.9 160.3 %shard_map.64 = bf16[128,4,1,128]{3,2,1,0:T(2,128)(2,1)} custom-call(bf16[3,4,2,2,8,128,128]{6,5,4,3,2,1,0:T(8,128)(2,1)} %bitcast.10, bf16[128,4,1,128]{3,2,1,0:T(2,128)(2,1)} %bitcast.12, s32[16,128]{1,0:T(8,128)} %concatenate.3.meta, f32[3,4,1,128]{3,2,1,0:T(1,128)} %reshape.14.bias), custom_call_target="tpu_custom_call" | custom-call | tf_op jit(solution)/shard_map/pallas_call | solution.py:394
  164.2 1.9 %copy.15 = bf16[1,65536]{1,0:T(2,128)(2,1)} copy(bf16[1,65536]{1,0:T(2,128)(2,1)} %bitcast.11) | data formatting | bytes 262144
  (2 shorter events, 0.0 us)

commit v4 on v3

--- a/solution.py
+++ b/solution.py
@@ -19,7 +19,7 @@
     return side * 2 + role % 2 if level == 0 else 4 + ((level - 1) * 2 + side) * 4 + role
 
 
-def layers_kernel(w_hbm, feat, meta, bias, out, inb, outb, wbuf, acta, actb, work,
+def layers_kernel(w_hbm, feat, row_in, live_in, col_in, bias, out, pack, meta, biasv, inb, outb, wbuf, acta, actb, work,
                   yab, yaf, sa, saz, ybf, sbz, sbx, ra, zra, zrb, rb, metav, colv, metas, cols,
                   wl_sem, ws_sem, wr_sem, ms_sem, mr_sem, cs_sem, cr_sem, loc_sem,
                   in_s, in_r, out_s, out_r, ag_s, ag_r,
@@ -73,6 +73,15 @@
         return pltpu.make_async_remote_copy(src_ref=src, dst_ref=dst, send_sem=ss, recv_sem=rs,
                                             device_id=d, device_id_type=MESH)
 
+    for r in range(4):
+        pack[:, r, :] = feat[:, r, 0, :]
+    for i in range(row_in.shape[0]):
+        meta[i, :] = row_in[i, 0, :]
+        meta[3 + i, :] = live_in[i, 0, :]
+        meta[8 + i, :] = col_in[i, 0, :]
+        for r in range(4):
+            biasv[i, r, 0, :] = bias[i, r * 128:(r + 1) * 128]
+
     barrier = pltpu.get_barrier_semaphore()
 
     def greet(k, d):
@@ -83,7 +92,7 @@
     for_half(greet)
     pl.semaphore_wait(barrier, 2 + HALF - 1)
 
-    for_half(lambda k, d: remote(feat.at[k], inb.at[flat], in_s, in_r, d).start())
+    for_half(lambda k, d: remote(pack.at[k], inb.at[flat], in_s, in_r, d).start())
 
     metav[me] = meta[pl.ds(0, 8), :]
     colv[plane] = meta[pl.ds(8, 8), :]
@@ -142,7 +151,7 @@
             ag(l, st, me, 1, partner).wait_send()
             ag(l, st, me, 2, partner).wait_send()
 
-    start_weights(0, 0, 2)
+    start_weights(0, 0, 4)
     for k, d, src in group:
         remote(meta.at[pl.ds(0, 8)], metav.at[src], ms_sem.at[k], mr_sem.at[k], d).wait_recv()
         meta_cp(k, d).wait_send()
@@ -152,11 +161,11 @@
     tables = (pltpu.make_async_copy(metav, metas, loc_sem.at[0]), pltpu.make_async_copy(colv, cols, loc_sem.at[1]))
     for cp in tables:
         cp.start()
-    inb[flat] = feat[flat]
-    lot = remote(feat.at[pl.ds(0, HALF - 1)], inb.at[pl.ds(0, HALF - 1)], in_s, in_r, partner)
+    inb[flat] = pack[flat]
+    lot = remote(pack.at[pl.ds(0, HALF - 1)], inb.at[pl.ds(0, HALF - 1)], in_s, in_r, partner)
     lot.wait_recv()
     for r in range(4):
-        rows = inb[:, r, 0, :].astype(f32).astype(bf16)
+        rows = inb[:, r, :]
         acta[0, me, r] = rows[:HA]
         actb[0, me, r] = rows[HA:]
     gather_start(0, 0)
@@ -165,10 +174,13 @@
     for cp in tables:
         cp.wait()
 
+    def bias_of(l, lo, n):
+        return biasv[l, lo:lo + n]
+
     def layer(l, carry):
         @pl.when(l == 0)
         def _():
-            start_weights(l, 2, 8)
+            start_weights(l, 4, 8)
 
         @pl.when(l > 0)
         def _():
@@ -280,7 +292,7 @@
                 saz[k] = acc.astype(bf16)
                 za(k).start()
             else:
-                acta[l + 1, me] = jnp.maximum(acc + bias[l], 0.0).astype(bf16)
+                acta[l + 1, me] = jnp.maximum(acc + bias_of(l, 0, 4), 0.0).astype(bf16)
 
         def b_step(level, role):
             for side, chain in ((0, UP), (1, DOWN)):
@@ -322,7 +334,7 @@
                 xb(n, xp).wait_recv()
             for lo, up, dn in ((0, 2, 5), (2, 3, 4)):
                 acc = ybf[7, 3, lo:lo + 2] + rb[l, up].astype(f32) + rb[l, dn].astype(f32)
-                actb[l + 1, me, lo:lo + 2] = jnp.maximum(acc + bias[l, lo:lo + 2], 0.0).astype(bf16)
+                actb[l + 1, me, lo:lo + 2] = jnp.maximum(acc + bias_of(l, lo, 2), 0.0).astype(bf16)
 
         a_acc(0)
         a_acc(2)
@@ -377,8 +389,8 @@
     lax.fori_loop(0, layers, layer, 0)
 
     for r in range(4):
-        outb[pl.ds(0, HA), r, 0, :] = acta[layers, me, r]
-        outb[pl.ds(HA, HB), r, 0, :] = actb[layers, me, r]
+        outb[pl.ds(0, HA), r, :] = acta[layers, me, r]
+        outb[pl.ds(HA, HB), r, :] = actb[layers, me, r]
     for_half(lambda k, d: remote(outb.at[k], out.at[flat], out_s, out_r, d).start())
     out[flat] = outb[flat]
     lot = remote(outb.at[pl.ds(0, HALF - 1)], out.at[pl.ds(0, HALF - 1)], out_s, out_r, partner)
@@ -386,19 +398,23 @@
     lot.wait_send()
 
 
-def run_layers(w, feat, meta, bias):
+def run_layers(w, feat, row, live, col, bias):
     layers = w.shape[0]
     bf16, f32, DMA = jnp.bfloat16, jnp.float32, pltpu.SemaphoreType.DMA
     pa, pb, hb = (4, HA, 128), (4, HB, 128), (2, HB, 128)
+    slabs = (HALF, 4, 128)
     vm = pl.BlockSpec(memory_space=pltpu.VMEM)
     return pl.pallas_call(
         layers_kernel,
-        out_shape=jax.ShapeDtypeStruct(feat.shape, bf16),
-        in_specs=[pl.BlockSpec(memory_space=pl.ANY), vm, vm, vm],
+        out_shape=jax.ShapeDtypeStruct(slabs, bf16),
+        in_specs=[pl.BlockSpec(memory_space=pl.ANY)] + [vm] * 5,
         out_specs=vm,
         scratch_shapes=[
-            pltpu.VMEM(feat.shape, bf16),
-            pltpu.VMEM(feat.shape, bf16),
+            pltpu.VMEM(slabs, bf16),
+            pltpu.VMEM((16, 128), jnp.int32),
+            pltpu.VMEM((layers, 4, 1, 128), f32),
+            pltpu.VMEM(slabs, bf16),
+            pltpu.VMEM(slabs, bf16),
             pltpu.VMEM((layers, 4, NZ, NXC, 128, 128), bf16),
             pltpu.VMEM((layers + 1, 4) + pa, bf16),
             pltpu.VMEM((layers + 1, 4) + pb, bf16),
@@ -429,16 +445,13 @@
         ],
         compiler_params=pltpu.CompilerParams(
             collective_id=0, has_side_effects=True, vmem_limit_bytes=60 * 1024 * 1024),
-    )(w, feat, meta, bias)
+    )(w, feat, row, live, col, bias)
 
 
 def local(features, link_weight, link_row, link_col, link_live, bias):
-    two = jnp.zeros((2, 128), jnp.int32)
-    five = jnp.zeros((5, 128), jnp.int32)
-    meta = jnp.concatenate([link_row[:, 0], link_live[:, 0], two, link_col[:, :, 0], five], axis=0)
     layers = bias.shape[0]
-    res = run_layers(link_weight.reshape(layers, NXC, 2, 2, NZ, 128, 128), features.reshape(HALF, 4, 1, 128), meta,
-                     bias.reshape(layers, 4, 1, 128))
+    res = run_layers(link_weight.reshape(layers, NXC, 2, 2, NZ, 128, 128), features.reshape(HALF, 4, 1, 128),
+                     link_row, link_live, link_col.transpose(0, 2, 1), bias)
     return res.reshape(features.shape)
 
 

time: 166 us -> 156 us (0.940)
  Pallas kernels: 160 us -> 154 us
  local copies, waits for them, and re-layouts: 5.82 us -> 1.66 us
    pallas_call x1, Pallas kernels: 160 us -> 154 us  [run_layers(): pl.pallas_call(layers_kernel, out_shape=jax.ShapeDtypeStruct(slabs, bf16)...]
    unnamed x3 -> x0, local copies, waits for them, and re-layouts: 3.3 us -> none
where the time goes in v4:
time: 156 us; the launch traced here: 155 us
  Pallas kernels  154 us (99%)
  local copies, waits for them, and re-layouts  1.66 us (1%)
    pallas_call x1, Pallas kernels, run_layers(): pl.pallas_call(layers_kernel, out_shape=jax.ShapeDtypeStruct(slabs, bf16)...  154 us

profile of v4, /device:TPU:1, one launch (start us, length us, event | category | flops | bytes accessed | tf_op | source)
XLA Modules:
  0.0 155.4 jit_solution(10751954859028407823)
XLA Ops:
  0.0 153.8 %shard_map.64 = bf16[128,4,128]{2,1,0:T(4,128)(2,1)} custom-call(bf16[3,4,2,2,8,128,128]{6,5,4,3,2,1,0:T(8,128)(2,1)} %bitcast.3, bf16[128,4,1,128]{3,2,1,0:T(2,128)(2,1)} %bitcast.4, s32[3,1,128]{2,1,0:T(1,128)} %row_in.1, s32[3,1,128]{2,1,0:T(1,128)} %live_in.1, s32[3,1,128]{2,1,0:T(1,128)} %bitcast.5, f32[3,512]{1,0:T(4,128)} %bias.1), custom_call_target="tpu_custom_call" | custom-call | tf_op jit(solution)/shard_map/pallas_call | solution.py:407
  153.8 1.7 %reshape.11 = bf16[1,65536]{1,0:T(2,128)(2,1)} reshape(bf16[128,4,128]{2,1,0:T(4,128)(2,1)} %shard_map.64) | data formatting | bytes 262144 | tf_op jit(solution)/shard_map/reshape | solution.py:455

commit v5 on v0

v5 whole, which is shorter than its diff:
```python
import jax
import jax.numpy as jnp
from jax import lax
from jax.experimental import pallas as pl
from jax.experimental.pallas import tpu as pltpu
from jax.sharding import PartitionSpec as P

MESH = pl.DeviceIdType.MESH
NXC, NZ = 4, 8
NY = 2 * NZ
HALF = 2 * NXC * NY
LAYERS = 3
STREAMS = ((0, 48), (0, 32), (1, 48))
OFFSET = tuple(sum(m for _, m in STREAMS[:i]) for i in range(len(STREAMS)))
UP = (0, 1, 3, 5)
DOWN = (0, 2, 4, 6)
JOIN = {0: (1, 1), 1: (1, 3), 2: (1, 4), 3: (1, 5), 4: (1, 6), 5: (1, 7), 6: (1, 7)}
FIRST, EARLY = 4, 6
SEGS = (((0,), (1,), (2,), (3,), (4,), (5,), (6,), (7,)), ((0,), (1, 2), (3, 4), (5, 6, 7)))
AGS, FWD, WORK, COL, S1, IM, AC, TO, FIN, B0, B1, B2, B3, BF, BI, BA, BO = range(17)
ORDER = (
    (AGS, 0, 0, 0), (AGS, 0, 2, 0), (AGS, 0, 1, 0), (FWD, 0, 0, 0), (FWD, 0, 2, 0), (WORK, 0, 0, 0), (COL, 0, 0, 0),
    (FWD, 0, 1, 0), (S1, 0, 0, 0), (COL, 0, 0, 1), (S1, 0, 0, 1), (WORK, 0, 2, 0), (COL, 0, 2, 0), (B0, 0, 2, 0),
    (COL, 0, 2, 1), (B0, 0, 2, 1), (COL, 0, 0, 2), (S1, 0, 0, 2), (COL, 0, 0, 3), (IM, 0, 0, 3), (IM, 0, 0, 1),
    (B0, 0, 2, 2), (IM, 0, 0, 2), (COL, 0, 2, 2), (B1, 0, 2, 5), (COL, 0, 0, 4), (AC, 0, 0, 0), (B1, 0, 2, 4),
    (B1, 0, 2, 2), (S1, 0, 0, 3), (B0, 0, 2, 3), (COL, 0, 2, 3), (COL, 0, 2, 4), (B1, 0, 2, 0), (AC, 0, 0, 1),
    (IM, 0, 0, 0), (S1, 0, 0, 4), (IM, 0, 0, 4), (WORK, 0, 1, 0), (COL, 0, 1, 0), (IM, 0, 1, 0), (COL, 0, 1, 1),
    (COL, 0, 0, 5), (S1, 0, 1, 1), (COL, 0, 2, 5), (S1, 0, 1, 0), (AC, 0, 0, 2), (COL, 0, 1, 2), (S1, 0, 1, 2),
    (B2, 0, 2, 2), (B2, 0, 2, 5), (S1, 0, 0, 5), (B1, 0, 2, 1), (COL, 0, 1, 3), (IM, 0, 1, 1), (COL, 0, 1, 4),
    (COL, 0, 1, 5), (COL, 0, 0, 6), (IM, 0, 1, 4), (S1, 0, 1, 3), (TO, 0, 0, 0), (B2, 0, 2, 0), (COL, 0, 2, 6),
    (S1, 0, 0, 6), (AC, 0, 0, 3), (AC, 0, 0, 4), (B2, 0, 2, 4), (COL, 0, 1, 6), (B1, 0, 2, 7), (B1, 0, 2, 3),
    (B1, 0, 2, 6), (IM, 0, 0, 5), (IM, 0, 1, 2), (B3, 0, 2, 2), (B3, 0, 2, 5), (COL, 0, 1, 7), (COL, 0, 0, 7),
    (TO, 0, 0, 2), (AC, 0, 1, 0), (AC, 0, 1, 1), (IM, 0, 1, 7), (AC, 0, 1, 2), (COL, 0, 2, 7), (TO, 0, 0, 1),
    (AC, 0, 0, 5), (IM, 0, 1, 3), (B2, 0, 2, 1), (B3, 0, 2, 4), (IM, 0, 1, 5), (S1, 0, 0, 7), (B3, 0, 2, 0),
    (S1, 0, 1, 6), (B2, 0, 2, 7), (IM, 0, 0, 6), (B2, 0, 2, 3), (S1, 0, 1, 4), (B2, 0, 2, 6), (IM, 0, 0, 7),
    (AC, 0, 1, 3), (TO, 0, 1, 0), (S1, 0, 1, 7), (AC, 0, 0, 6), (TO, 0, 0, 3), (S1, 0, 1, 5), (TO, 0, 1, 2),
    (TO, 0, 0, 4), (IM, 0, 1, 6), (B3, 0, 2, 1), (BF, 0, 2, 0), (AC, 0, 0, 7), (AC, 0, 1, 6), (B3, 0, 2, 7),
    (B3, 0, 2, 3), (AC, 0, 1, 4), (B3, 0, 2, 6), (TO, 0, 1, 1), (AC, 0, 1, 7), (TO, 0, 0, 5), (TO, 0, 0, 6),
    (AC, 0, 1, 5), (BI, 0, 2, 0), (BA, 0, 2, 0), (BO, 0, 2, 0), (TO, 0, 1, 4), (BI, 0, 2, 1), (BA, 0, 2, 1),
    (TO, 0, 1, 3), (FIN, 0, 0, 0), (AGS, 1, 0, 0), (TO, 0, 1, 6), (TO, 0, 1, 5), (FIN, 0, 2, 0), (AGS, 1, 2, 0),
    (FWD, 1, 0, 0), (WORK, 1, 0, 0), (COL, 1, 0, 0), (S1, 1, 0, 0), (COL, 1, 0, 1), (S1, 1, 0, 1), (FWD, 1, 2, 0),
    (S1, 1, 0, 2), (FIN, 0, 1, 0), (AGS, 1, 1, 0), (COL, 1, 0, 2), (IM, 1, 0, 3), (IM, 1, 0, 1), (IM, 1, 0, 2),
    (S1, 1, 0, 3), (IM, 1, 0, 0), (WORK, 1, 2, 0), (COL, 1, 2, 0), (B0, 1, 2, 0), (COL, 1, 2, 1), (AC, 1, 0, 0),
    (B1, 1, 2, 5), (B0, 1, 2, 1), (B0, 1, 2, 2), (COL, 1, 2, 2), (FWD, 1, 1, 0), (AC, 1, 0, 2), (B1, 1, 2, 4),
    (B1, 1, 2, 2), (AC, 1, 0, 1), (S1, 1, 0, 4), (IM, 1, 0, 4), (B1, 1, 2, 3), (B0, 1, 2, 3), (WORK, 1, 1, 0),
    (COL, 1, 1, 0), (IM, 1, 1, 0), (B1, 1, 2, 0), (S1, 1, 1, 0), (COL, 1, 1, 1), (S1, 1, 1, 1), (S1, 1, 1, 2),
    (AC, 1, 0, 3), (B2, 1, 2, 5), (COL, 1, 1, 2), (IM, 1, 1, 4), (TO, 1, 0, 0), (IM, 1, 1, 1), (IM, 1, 1, 3),
    (B1, 1, 2, 1), (S1, 1, 1, 4), (B1, 1, 2, 6), (B2, 1, 2, 2), (IM, 1, 1, 2), (TO, 1, 0, 2), (S1, 1, 1, 3),
    (B2, 1, 2, 4), (B2, 1, 2, 3), (AC, 1, 0, 4), (COL, 1, 0, 3), (AC, 1, 1, 0), (B2, 1, 2, 0), (S1, 1, 0, 6),
    (S1, 1, 0, 5), (AC, 1, 1, 2), (COL, 1, 2, 3), (AC, 1, 1, 1), (TO, 1, 0, 1), (S1, 1, 0, 7), (B3, 1, 2, 5),
    (COL, 1, 1, 3), (IM, 1, 1, 7), (IM, 1, 0, 6), (B3, 1, 2, 2), (S1, 1, 1, 6), (IM, 1, 1, 5), (AC, 1, 1, 4),
    (B2, 1, 2, 6), (B1, 1, 2, 7), (B2, 1, 2, 1), (TO, 1, 0, 4), (IM, 1, 0, 5), (AC, 1, 1, 3), (B3, 1, 2, 3),
    (B3, 1, 2, 4), (S1, 1, 1, 7), (TO, 1, 1, 0), (IM, 1, 0, 7), (IM, 1, 1, 6), (TO, 1, 1, 2), (B3, 1, 2, 0),
    (AC, 1, 0, 6), (AC, 1, 0, 5), (TO, 1, 0, 3), (B3, 1, 2, 6), (AC, 1, 1, 6), (S1, 1, 1, 5), (AC, 1, 0, 7),
    (B2, 1, 2, 7), (B3, 1, 2, 1), (AC, 1, 1, 7), (TO, 1, 1, 1), (TO, 1, 1, 4), (BF, 1, 2, 0), (TO, 1, 0, 6),
    (BI, 1, 2, 1), (TO, 1, 0, 5), (AC, 1, 1, 5), (B3, 1, 2, 7), (BI, 1, 2, 0), (TO, 1, 1, 6), (TO, 1, 1, 3),
    (BA, 1, 2, 1), (BA, 1, 2, 0), (FIN, 1, 0, 0), (AGS, 2, 0, 0), (BO, 1, 2, 0), (TO, 1, 1, 5), (FIN, 1, 2, 0),
    (AGS, 2, 2, 0), (FWD, 2, 0, 0), (FIN, 1, 1, 0), (AGS, 2, 1, 0), (WORK, 2, 0, 0), (COL, 2, 0, 0), (S1, 2, 0, 0),
    (FWD, 2, 2, 0), (COL, 2, 0, 1), (S1, 2, 0, 1), (S1, 2, 0, 2), (COL, 2, 0, 2), (WORK, 2, 2, 0), (COL, 2, 2, 0),
    (B0, 2, 2, 0), (COL, 2, 2, 1), (FWD, 2, 1, 0), (B1, 2, 2, 5), (B0, 2, 2, 1), (IM, 2, 0, 3), (IM, 2, 0, 1),
    (B0, 2, 2, 2), (IM, 2, 0, 2), (B1, 2, 2, 4), (COL, 2, 2, 2), (AC, 2, 0, 0), (B1, 2, 2, 2), (S1, 2, 0, 3),
    (IM, 2, 0, 0), (B1, 2, 2, 3), (B0, 2, 2, 3), (S1, 2, 0, 4), (WORK, 2, 1, 0), (COL, 2, 1, 0), (S1, 2, 1, 0),
    (COL, 2, 1, 1), (S1, 2, 1, 1), (IM, 2, 1, 0), (COL, 2, 1, 2), (B1, 2, 2, 0), (IM, 2, 1, 4), (S1, 2, 1, 2),
    (S1, 2, 1, 3), (B2, 2, 2, 5), (AC, 2, 0, 2), (B1, 2, 2, 1), (IM, 2, 1, 2), (B1, 2, 2, 6), (S1, 2, 1, 4),
    (B2, 2, 2, 2), (AC, 2, 0, 1), (COL, 2, 1, 3), (B2, 2, 2, 3), (IM, 2, 1, 7), (TO, 2, 0, 0), (COL, 2, 0, 3),
    (AC, 2, 1, 0), (AC, 2, 1, 1), (B2, 2, 2, 0), (AC, 2, 0, 4), (S1, 2, 0, 6), (AC, 2, 0, 3), (B2, 2, 2, 4),
    (COL, 2, 2, 3), (AC, 2, 1, 3), (AC, 2, 1, 2), (B3, 2, 2, 5), (IM, 2, 1, 1), (B2, 2, 2, 6), (B3, 2, 2, 2),
    (S1, 2, 0, 5), (B1, 2, 2, 7), (B2, 2, 2, 1), (IM, 2, 0, 5), (B3, 2, 2, 3), (TO, 2, 0, 2), (S1, 2, 0, 7),
    (IM, 2, 0, 7), (TO, 2, 1, 0), (S1, 2, 1, 5), (B3, 2, 2, 4), (TO, 2, 0, 1), (S1, 2, 1, 6), (IM, 2, 0, 6),
    (IM, 2, 1, 3), (B3, 2, 2, 0), (IM, 2, 0, 4), (AC, 2, 0, 6), (TO, 2, 1, 2), (B3, 2, 2, 6), (S1, 2, 1, 7),
    (AC, 2, 1, 4), (B3, 2, 2, 1), (B2, 2, 2, 7), (AC, 2, 0, 5), (IM, 2, 1, 5), (AC, 2, 0, 7), (TO, 2, 1, 1),
    (AC, 2, 1, 5), (AC, 2, 1, 6), (TO, 2, 0, 3), (IM, 2, 1, 6), (BF, 2, 2, 0), (TO, 2, 0, 4), (BI, 2, 2, 1),
    (AC, 2, 1, 7), (BI, 2, 2, 0), (TO, 2, 1, 4), (B3, 2, 2, 7), (TO, 2, 1, 3), (TO, 2, 0, 5), (BA, 2, 2, 1),
    (TO, 2, 0, 6), (TO, 2, 1, 6), (TO, 2, 1, 5), (BA, 2, 2, 0), (BO, 2, 2, 0), (FIN, 2, 0, 0), (FIN, 2, 2, 0),
    (FIN, 2, 1, 0),
)


def bslot(side, level, role):
    return side * 2 + role % 2 if level == 0 else 4 + ((level - 1) * 2 + side) * 4 + role


def scratch(layers):
    bf16, f32, i32, DMA, V = jnp.bfloat16, jnp.float32, jnp.int32, pltpu.SemaphoreType.DMA, pltpu.VMEM
    slabs = (HALF, 4, 128)
    res = dict(
        pack=V(slabs, bf16), inb=V(slabs, bf16), outb=V(slabs, bf16),
        meta=V((16, 128), i32), biasv=V((layers, 4, 1, 128), f32),
        wbuf=V((layers, 4, NZ, NXC, 128, 128), bf16),
        metav=V((4, 8, 128), i32), colv=V((NXC * NZ, 8, 128), i32),
        metas=pltpu.SMEM((4, 8, 128), i32), cols=pltpu.SMEM((NXC * NZ, 8, 128), i32),
        wl_sem=DMA((layers, NZ)), ws_sem=DMA((layers,)), wr_sem=DMA((layers, NZ)),
        ms_sem=DMA((3,)), mr_sem=DMA((3,)), cs_sem=DMA, cr_sem=DMA, loc_sem=DMA((2,)),
        in_s=DMA, in_r=DMA, out_s=DMA, out_r=DMA,
    )
    for i, (kind, m) in enumerate(STREAMS):
        p = (4, m, 128)
        res.update({f"act{i}": V((layers + 1, 4) + p, bf16), f"work{i}": V((4,) + p, bf16),
                    f"ag_s{i}": DMA((layers, 3)), f"ag_r{i}": DMA((layers, 3))})
        if kind == 0:
            res.update({f"yb{i}": V((NZ, 2) + p, bf16), f"yf{i}": V((NZ, 2) + p, f32),
                        f"sx{i}": V((NZ,) + p, bf16), f"sz{i}": V((NZ - 1,) + p, bf16),
                        f"rx{i}": V((layers, 3, NZ) + p, bf16), f"rz{i}": V((layers, NZ - 1) + p, bf16),
                        f"sx_sem{i}": DMA((layers,)), f"rx_sem{i}": DMA((layers, 3, NZ)),
                        f"sz_sem{i}": DMA((layers,)), f"rz_sem{i}": DMA((layers, NZ - 1))})
        else:
            h = (2, m, 128)
            res.update({f"yf{i}": V((NZ, 4) + p, f32),
                        f"sx{i}": V((6,) + h, bf16), f"sz{i}": V((28,) + p, bf16),
                        f"rx{i}": V((layers, 6) + h, bf16), f"rz{i}": V((layers, 28) + p, bf16),
                        f"sx_sem{i}": DMA((layers,)), f"rx_sem{i}": DMA((layers, 6)),
                        f"sz_sem{i}": DMA((layers,)), f"rz_sem{i}": DMA((layers, 28))})
    return res


def layers_kernel(w_hbm, feat, row_in, live_in, col_in, bias, out, *refs):
    f32, bf16 = jnp.float32, jnp.bfloat16
    s = dict(zip(scratch(LAYERS), refs))
    pack, inb, outb, meta, biasv, wbuf = (s[n] for n in ("pack", "inb", "outb", "meta", "biasv", "wbuf"))
    metav, colv, metas, cols = (s[n] for n in ("metav", "colv", "metas", "cols"))
    nx, ny, im = lax.axis_index("nx"), lax.axis_index("ny"), lax.axis_index("img")
    x, c = nx // 2, nx % 2
    yl, z = ny // NZ, ny % NZ
    me = yl * 2 + c
    plane = x * NZ + z
    flat = nx * NY + ny
    layers = LAYERS

    def dev(xx, cc, yy, zz, ii):
        return (xx * 2 + cc, yy * NZ + zz, ii)

    partner = dev(x, 1 - c, yl, z, im)
    near = dev(x, c, 1 - yl, z, im)
    diag = dev(x, 1 - c, 1 - yl, z, im)
    im_up = (im + yl) % 2
    im_dn = (im + 1 - yl) % 2
    x1, x2, x3 = (x + 1) % NXC, (x + 2) % NXC, (x + 3) % NXC
    xp, xm = dev(x1, c, yl, z, im), dev(x3, c, yl, z, im)

    def along_z(hops):
        return dev(x, c, yl, (z + NZ + hops) % NZ, im)

    def plus(k):
        return k % 2 == 1 or k == 0

    def col_z(k):
        far = 4 - (k + 1) // 2
        return (z + NZ + jnp.where(k % 2 == 1, far, -far)) % NZ

    def for_half(fn):
        for b in range(1, NY):
            fn(nx * NY + (ny + b) % NY, (nx, (ny + b) % NY, im))

        def rows(a, carry):
            n = (nx + a) % (2 * NXC)
            for b in range(NY):
                fn(n * NY + (ny + b) % NY, (n, (ny + b) % NY, im))
            return carry

        lax.fori_loop(1, 2 * NXC, rows, 0)

    def for_plane(fn):
        def step(j, carry):
            fn(j, dev((x + j // NZ) % NXC, c, yl, (z + j) % NZ, im))
            return carry

        lax.fori_loop(1, NXC * NZ, step, 0)

    def remote(src, dst, ss, rs, d):
        return pltpu.make_async_remote_copy(src_ref=src, dst_ref=dst, send_sem=ss, recv_sem=rs,
                                            device_id=d, device_id_type=MESH)

    barrier = pltpu.get_barrier_semaphore()

    def greet(k, d):
        pl.semaphore_signal(barrier, inc=1, device_id=d, device_id_type=MESH)

    for cc in (0, 1):
        greet(0, dev(x, cc, 1 - yl, z, 1 - im))
    for_half(greet)
    for r in range(4):
        pack[:, r, :] = feat[:, r, 0, :]
    for i in range(layers):
        meta[i, :] = row_in[i, 0, :]
        meta[3 + i, :] = live_in[i, 0, :]
        meta[8 + i, :] = col_in[i, 0, :]
        for r in range(4):
            biasv[i, r, 0, :] = bias[i, r * 128:(r + 1) * 128]
    metav[me] = meta[pl.ds(0, 8), :]
    colv[plane] = meta[pl.ds(8, 8), :]
    pl.semaphore_wait(barrier, 2 + HALF - 1)

    for_half(lambda k, d: remote(pack.at[k], inb.at[flat], s["in_s"], s["in_r"], d).start())

    def meta_cp(k, d):
        return remote(meta.at[pl.ds(0, 8)], metav.at[me], s["ms_sem"].at[k], s["mr_sem"].at[k], d)

    group = ((0, partner, yl * 2 + 1 - c), (1, near, (1 - yl) * 2 + c), (2, diag, (1 - yl) * 2 + 1 - c))
    for k, d, _ in group:
        meta_cp(k, d).start()
    for_plane(lambda j, d: remote(meta.at[pl.ds(8, 8)], colv.at[plane], s["cs_sem"], s["cr_sem"], d).start())

    def start_weights(l, lo, hi):
        def step(k, carry):
            zz = col_z(k)

            def send(x0, n, cc, yy, ii):
                remote(w_hbm.at[l, pl.ds(x0, n), cc, yy, zz], wbuf.at[l, me, k, pl.ds(x0, n)],
                       s["ws_sem"].at[l], s["wr_sem"].at[l, k], dev(x, cc, yy, z, ii)).start()

            for cc in (0, 1):
                send(0, 2, cc, 1 - yl, im_up)
                send(2, 2, cc, 1 - yl, im_dn)
            send(0, 4, 1 - c, yl, im)
            pltpu.make_async_copy(w_hbm.at[l, :, c, yl, zz], wbuf.at[l, me, k], s["wl_sem"].at[l, k]).start()
            return carry

        lax.fori_loop(lo, hi, step, 0)

    def wait_weights(l, k):
        pltpu.make_async_copy(w_hbm.at[l, :, c, yl, 0], wbuf.at[l, me, k], s["wl_sem"].at[l, k]).wait()
        three = wbuf.at[l, pl.ds(0, 3), k]
        remote(three, three, s["ws_sem"].at[l], s["wr_sem"].at[l, k], partner).wait_recv()

    start_weights(0, 0, FIRST)
    for k, d, src in group:
        remote(meta.at[pl.ds(0, 8)], metav.at[src], s["ms_sem"].at[k], s["mr_sem"].at[k], d).wait_recv()
        meta_cp(k, d).wait_send()
    lot = colv.at[pl.ds(0, NXC * NZ - 1)]
    lot = remote(lot, lot, s["cs_sem"], s["cr_sem"], partner)
    lot.wait_recv()
    lot.wait_send()
    tables = (pltpu.make_async_copy(metav, metas, s["loc_sem"].at[0]),
              pltpu.make_async_copy(colv, cols, s["loc_sem"].at[1]))
    for cp in tables:
        cp.start()
    inb[flat] = pack[flat]
    lot = remote(pack.at[pl.ds(0, HALF - 1)], inb.at[pl.ds(0, HALF - 1)], s["in_s"], s["in_r"], partner)
    lot.wait_recv()
    for r in range(4):
        rows = inb[:, r, :]
        for i, (_, m) in enumerate(STREAMS):
            s[f"act{i}"][0, me, r] = rows[OFFSET[i]:OFFSET[i] + m]

    def ag(l, i, src, slot, d):
        ref = s[f"act{i}"].at[l, src]
        return remote(ref, ref, s[f"ag_s{i}"].at[l, slot], s[f"ag_r{i}"].at[l, slot], d)

    def ags(l, i, _):
        ag(l, i, me, 0, near).start()
        ag(l, i, me, 1, partner).start()

    def fwd(l, i, _):
        ag(l, i, (1 - yl) * 2 + c, 0, near).wait_recv()
        ag(l, i, (1 - yl) * 2 + c, 2, partner).start()

    def sent(l, i):
        for slot in range(3):
            ag(l, i, me, slot, partner).wait_send()
        for a in "xz":
            ref = s[f"r{a}{i}"].at[l]
            remote(ref, ref, s[f"s{a}_sem{i}"].at[l], s["in_r"], partner).wait_send()

    def work(l, i, _):
        ag(l, i, yl * 2 + 1 - c, 1, partner).wait_recv()
        ag(l, i, (1 - yl) * 2 + 1 - c, 2, partner).wait_recv()
        if l > 0:
            sent(l - 1, i)
        for src in range(4):
            s[f"work{i}"][src] = s[f"act{i}"][l, src]

    arrived = set()

    def col(l, i, seg):
        kind, _ = STREAMS[i]
        ks = SEGS[min(l, 1)][seg]
        for k in ks:
            if (l, k) not in arrived:
                arrived.add((l, k))
                wait_weights(l, k)
        held, yf = s[f"work{i}"], s[f"yf{i}"]

        def product(k, xx, zz):
            dest = (xx * 2 + c) * NY + yl * NZ + zz
            parts = [None] * 4
            for src in range(4):
                at = (x * 2 + src % 2) * NY + (src // 2) * NZ + z
                row, live, place = metas[src, l, dest], metas[src, 3 + l, dest], cols[xx * NZ + zz, l, at]
                term = jnp.dot(held[src, row], wbuf[l, src, k, xx], preferred_element_type=f32)
                key = jnp.where(live == 1, place, 4)
                for q in range(4):
                    mine = jnp.where(key == q, term, jnp.zeros_like(term))
                    parts[q] = mine if src == 0 else parts[q] + mine
            return parts

        def step(t, carry):
            k, p = t // 2, t % 2
            zz = col_z(k)
            up = jnp.where(jnp.logical_or(k % 2 == 1, k == 0), 1, 0)
            near_x = jnp.where(up == 1, x1, x3)
            far_x = jnp.where(up == 1, x3, x1)
            one = product(k, jnp.where(p == 0, x2, far_x), zz)
            two = product(k, jnp.where(p == 0, near_x, x), zz)
            for q in range(4):
                a, b = one[q], two[q]
                if kind == 0:
                    s[f"yb{i}"][k, p, q] = a.astype(bf16)
                    yf[k, p, q] = b
                else:
                    yf[k, p * (1 + up), q] = a
                    yf[k, 3 * p + (1 - p) * (2 - up), q] = b
            return carry

        lax.fori_loop(2 * ks[0], 2 * ks[-1] + 2, step, 0)

    def xa(l, i, k, n, src, d):
        return remote(src, s[f"rx{i}"].at[l, n, k], s[f"sx_sem{i}"].at[l], s[f"rx_sem{i}"].at[l, n, k], d)

    def s1(l, i, k):
        xa(l, i, k, 0, s[f"yb{i}"].at[k, 0], xp if plus(k) else xm).start()

    def imm(l, i, k):
        xa(l, i, k, 1, s[f"yb{i}"].at[k, 1], xm if plus(k) else xp).start()

    def acc(l, i, k):
        xa(l, i, k, 0, s[f"sx{i}"].at[k], xp).wait_recv()
        s[f"sx{i}"][k] = (s[f"yf{i}"][k, 0] + s[f"rx{i}"][l, 0, k].astype(f32)).astype(bf16)
        xa(l, i, k, 2, s[f"sx{i}"].at[k], xp if plus(k) else xm).start()

    def za(l, i, k):
        hops = JOIN[k][0]
        return remote(s[f"sz{i}"].at[k], s[f"rz{i}"].at[l, k], s[f"sz_sem{i}"].at[l], s[f"rz_sem{i}"].at[l, k],
                      along_z(hops if plus(k) else -hops))

    def total(l, i, k):
        for n in (1, 2):
            xa(l, i, k, n, s[f"sx{i}"].at[k], xp).wait_recv()
        val = (s[f"yf{i}"][k, 1] + s[f"rx{i}"][l, 1, k].astype(f32)) + s[f"rx{i}"][l, 2, k].astype(f32)
        for j in range(7):
            if JOIN[j][1] == k:
                za(l, i, j).wait_recv()
                val = val + s[f"rz{i}"][l, j].astype(f32)
        if k < 7:
            s[f"sz{i}"][k] = val.astype(bf16)
            za(l, i, k).start()
        else:
            s[f"act{i}"][l + 1, me] = jnp.maximum(val + biasv[l], 0.0).astype(bf16)

    def zb(l, i, side, level, role):
        n = bslot(side, level, role)
        return remote(s[f"sz{i}"].at[n], s[f"rz{i}"].at[l, n], s[f"sz_sem{i}"].at[l], s[f"rz_sem{i}"].at[l, n],
                      along_z(-1 if side else 1))

    def b_step(l, i, level, side, role):
        n = bslot(side, level, role)
        val = s[f"yf{i}"][(UP, DOWN)[side][level], role]
        if level > 1 or (level == 1 and role // 2 == side):
            zb(l, i, side, level - 1, role).wait_recv()
            val = val + s[f"rz{i}"][l, bslot(side, level - 1, role)].astype(f32)
        s[f"sz{i}"][n] = val.astype(bf16)
        zb(l, i, side, level, role).start()

    def xb(l, i, n, d):
        return remote(s[f"sx{i}"].at[n], s[f"rx{i}"].at[l, n], s[f"sx_sem{i}"].at[l], s[f"rx_sem{i}"].at[l, n], d)

    def b_sum(l, i, role):
        val = s[f"yf{i}"][7, role]
        for side in (0, 1):
            zb(l, i, side, 3, role).wait_recv()
            val = val + s[f"rz{i}"][l, bslot(side, 3, role)].astype(f32)
        return val

    def b_far(l, i, _):
        val = b_sum(l, i, 0)
        for n, d in ((0, xp), (1, xm)):
            s[f"sx{i}"][n] = val[2 * n:2 * n + 2].astype(bf16)
            xb(l, i, n, d).start()

    def b_imm(l, i, side):
        val = b_sum(l, i, 1 + side)
        n, hi, lo = 3 + 2 * side, 2 - 2 * side, 2 * side
        s[f"sx{i}"][n] = val[hi:hi + 2].astype(bf16)
        xb(l, i, n, xm if side else xp).start()
        s[f"yf{i}"][7, 1 + side, lo:lo + 2] = val[lo:lo + 2]

    def b_acc(l, i, side):
        n, lo = 2 + 2 * side, 2 * side
        xb(l, i, side, xp).wait_recv()
        s[f"sx{i}"][n] = (s[f"yf{i}"][7, 1 + side, lo:lo + 2] + s[f"rx{i}"][l, side].astype(f32)).astype(bf16)
        xb(l, i, n, xm if side else xp).start()

    def b_own(l, i, _):
        s[f"yf{i}"][7, 3] = b_sum(l, i, 3)

    def fin(l, i, _):
        if STREAMS[i][0] == 0:
            total(l, i, 7)
            return
        for n in range(2, 6):
            xb(l, i, n, xp).wait_recv()
        for lo, a, b in ((0, 2, 5), (2, 3, 4)):
            val = s[f"yf{i}"][7, 3, lo:lo + 2] + s[f"rx{i}"][l, a].astype(f32) + s[f"rx{i}"][l, b].astype(f32)
            s[f"act{i}"][l + 1, me, lo:lo + 2] = jnp.maximum(val + biasv[l, lo:lo + 2], 0.0).astype(bf16)

    steps = {AGS: ags, FWD: fwd, WORK: work, COL: col, S1: s1, IM: imm, AC: acc, TO: total, FIN: fin,
             B0: lambda l, i, r: b_step(l, i, 0, r // 2, r), BF: b_far, BI: b_imm, BA: b_acc, BO: b_own}
    for level, name in ((1, B1), (2, B2), (3, B3)):
        steps[name] = lambda l, i, a, level=level: b_step(l, i, level, a // 4, a % 4)
    count = {}
    tables_held = False
    for name, l, i, arg in ORDER:
        if name == COL and not tables_held:
            tables_held = True
            for cp in tables:
                cp.wait()
        steps[name](l, i, arg)
        if name in (AGS, FWD):
            count[name, l] = count.get((name, l), 0) + 1
            if count[name, l] == len(STREAMS):
                if name == AGS:
                    start_weights(l, EARLY if l else FIRST, NZ)
                elif l < layers - 1:
                    start_weights(l + 1, 0, EARLY)

    for r in range(4):
        for i, (_, m) in enumerate(STREAMS):
            outb[pl.ds(OFFSET[i], m), r, :] = s[f"act{i}"][layers, me, r]
    for_half(lambda k, d: remote(outb.at[k], out.at[flat], s["out_s"], s["out_r"], d).start())
    out[flat] = outb[flat]
    lot.wait_send()
    for i in range(len(STREAMS)):
        sent(layers - 1, i)
    for l in range(layers):
        three = wbuf.at[l, pl.ds(0, 3)]
        remote(three, three, s["ws_sem"].at[l], s["wr_sem"].at[l, 0], partner).wait_send()
    lot = remote(outb.at[pl.ds(0, HALF - 1)], out.at[pl.ds(0, HALF - 1)], s["out_s"], s["out_r"], partner)
    lot.wait_recv()
    lot.wait_send()


def run_layers(w, feat, row, live, col, bias):
    vm = pl.BlockSpec(memory_space=pltpu.VMEM)
    return pl.pallas_call(
        layers_kernel,
        out_shape=jax.ShapeDtypeStruct((HALF, 4, 128), jnp.bfloat16),
        in_specs=[pl.BlockSpec(memory_space=pl.ANY)] + [vm] * 5,
        out_specs=vm,
        scratch_shapes=list(scratch(LAYERS).values()),
        compiler_params=pltpu.CompilerParams(
            collective_id=0, has_side_effects=True, vmem_limit_bytes=60 * 1024 * 1024),
    )(w, feat, row, live, col, bias)


def local(features, link_weight, link_row, link_col, link_live, bias):
    layers = bias.shape[0]
    res = run_layers(link_weight.reshape(layers, NXC, 2, 2, NZ, 128, 128), features.reshape(HALF, 4, 1, 128),
                     link_row, link_live, link_col.transpose(0, 2, 1), bias)
    return res.reshape(features.shape)


def solution(mesh):
    placed = (
        P(("nx", "ny", "img"), None),
        P(None, ("nx", "ny"), None, None, None),
        P(None, ("nx", "ny"), None),
        P(None, None, ("nx", "ny")),
        P(None, ("nx", "ny"), None),
        P(None, ("nx", "ny")),
    )
    return jax.shard_map(
        local, mesh=mesh, in_specs=placed, out_specs=P(("nx", "ny", "img"), None), check_vma=False
    )
```

time: 400 us -> 140 us (0.35)
  waiting for transfers between devices: 202 us -> 0 us
  Pallas kernels: 0 us -> 138 us
  blocking collectives: 121 us -> 0 us
  starting transfers between devices: 31.3 us -> 0 us
  matrix products: 29.6 us -> 0 us
  local copies, waits for them, and re-layouts: 11.8 us -> 1.66 us
  other arithmetic: 4.39 us -> 0 us
    all_to_all x3 -> x0, waiting for transfers between devices: 202 us -> none  [the longest x2 192 us: local(): lax.all_to_all(link_terms, ('nx', 'ny'), split_axis=0, concat_axis=0, til...]
    pallas_call x0 -> x1, Pallas kernels: none -> 138 us  [run_layers(): pl.pallas_call(layers_kernel, out_shape=jax.ShapeDtypeStruct((HALF, 4, 12...]
    all_to_all x2 -> x0, blocking collectives: 121 us -> none  [the longest x1 103 us: local(): lax.all_to_all(link_terms, ('nx', 'ny'), split_axis=0, concat_axis=0, til...]
    all_to_all x3 -> x0, starting transfers between devices: 31.3 us -> none  [the longest x2 16.5 us: local(): lax.all_to_all(link_terms, ('nx', 'ny'), split_axis=0, concat_axis=0, til...]
    dot_general x6 -> x0, matrix products: 29.6 us -> none  [the longest x3 18.3 us: link_products(): jnp.einsum('ier,ers->eis', gathered, masked, preferred_element_type=jnp.f...]
    gather x3 -> x0, local copies, waits for them, and re-layouts: 9.15 us -> none  [link_products(): gathered = jnp.take(blocks, row_ids, axis=1)]
  transfers between devices with their start and end apart: 3 -> 0, of which waited for: 3 -> 0; matrix products, arithmetic and copies ran while one was open for 0% -> 0% of each run, Pallas kernels for 0% -> 0%
where the time goes in v5:
time: 140 us
  Pallas kernels  138 us (99%)
  local copies, waits for them, and re-layouts  1.66 us (1%)
    pallas_call x1, Pallas kernels, run_layers(): pl.pallas_call(layers_kernel, out_shape=jax.ShapeDtypeStruct((HALF, 4, 12...  138 us

profile of v5, /device:TPU:1, one launch (start us, length us, event | category | flops | bytes accessed | tf_op | source)
XLA Modules:
  0.0 139.7 jit_solution(2180277708425488157)
XLA Ops:
  0.0 138.0 %shard_map.64 = bf16[128,4,128]{2,1,0:T(4,128)(2,1)} custom-call(bf16[3,4,2,2,8,128,128]{6,5,4,3,2,1,0:T(8,128)(2,1)} %bitcast.3, bf16[128,4,1,128]{3,2,1,0:T(2,128)(2,1)} %bitcast.4, s32[3,1,128]{2,1,0:T(1,128)} %row_in.1, s32[3,1,128]{2,1,0:T(1,128)} %live_in.1, s32[3,1,128]{2,1,0:T(1,128)} %bitcast.5, f32[3,512]{1,0:T(4,128)} %bias.1), custom_call_target="tpu_custom_call" | custom-call | tf_op jit(solution)/shard_map/pallas_call | solution.py:443
  138.0 1.7 %reshape.11 = bf16[1,65536]{1,0:T(2,128)(2,1)} reshape(bf16[128,4,128]{2,1,0:T(4,128)(2,1)} %shard_map.64) | data formatting | bytes 262144 | tf_op jit(solution)/shard_map/reshape | solution.py:458

commit v6 on v5

--- a/solution.py
+++ b/solution.py
@@ -10,69 +10,70 @@
 NY = 2 * NZ
 HALF = 2 * NXC * NY
 LAYERS = 3
-STREAMS = ((0, 48), (0, 32), (1, 48))
+STREAMS = ((0, 32), (0, 48), (1, 48))
 OFFSET = tuple(sum(m for _, m in STREAMS[:i]) for i in range(len(STREAMS)))
 UP = (0, 1, 3, 5)
 DOWN = (0, 2, 4, 6)
 JOIN = {0: (1, 1), 1: (1, 3), 2: (1, 4), 3: (1, 5), 4: (1, 6), 5: (1, 7), 6: (1, 7)}
-FIRST, EARLY = 4, 6
+FIRST = 2
+SPLIT = 5
 SEGS = (((0,), (1,), (2,), (3,), (4,), (5,), (6,), (7,)), ((0,), (1, 2), (3, 4), (5, 6, 7)))
 AGS, FWD, WORK, COL, S1, IM, AC, TO, FIN, B0, B1, B2, B3, BF, BI, BA, BO = range(17)
 ORDER = (
-    (AGS, 0, 0, 0), (AGS, 0, 2, 0), (AGS, 0, 1, 0), (FWD, 0, 0, 0), (FWD, 0, 2, 0), (WORK, 0, 0, 0), (COL, 0, 0, 0),
-    (FWD, 0, 1, 0), (S1, 0, 0, 0), (COL, 0, 0, 1), (S1, 0, 0, 1), (WORK, 0, 2, 0), (COL, 0, 2, 0), (B0, 0, 2, 0),
-    (COL, 0, 2, 1), (B0, 0, 2, 1), (COL, 0, 0, 2), (S1, 0, 0, 2), (COL, 0, 0, 3), (IM, 0, 0, 3), (IM, 0, 0, 1),
-    (B0, 0, 2, 2), (IM, 0, 0, 2), (COL, 0, 2, 2), (B1, 0, 2, 5), (COL, 0, 0, 4), (AC, 0, 0, 0), (B1, 0, 2, 4),
-    (B1, 0, 2, 2), (S1, 0, 0, 3), (B0, 0, 2, 3), (COL, 0, 2, 3), (COL, 0, 2, 4), (B1, 0, 2, 0), (AC, 0, 0, 1),
-    (IM, 0, 0, 0), (S1, 0, 0, 4), (IM, 0, 0, 4), (WORK, 0, 1, 0), (COL, 0, 1, 0), (IM, 0, 1, 0), (COL, 0, 1, 1),
-    (COL, 0, 0, 5), (S1, 0, 1, 1), (COL, 0, 2, 5), (S1, 0, 1, 0), (AC, 0, 0, 2), (COL, 0, 1, 2), (S1, 0, 1, 2),
-    (B2, 0, 2, 2), (B2, 0, 2, 5), (S1, 0, 0, 5), (B1, 0, 2, 1), (COL, 0, 1, 3), (IM, 0, 1, 1), (COL, 0, 1, 4),
-    (COL, 0, 1, 5), (COL, 0, 0, 6), (IM, 0, 1, 4), (S1, 0, 1, 3), (TO, 0, 0, 0), (B2, 0, 2, 0), (COL, 0, 2, 6),
-    (S1, 0, 0, 6), (AC, 0, 0, 3), (AC, 0, 0, 4), (B2, 0, 2, 4), (COL, 0, 1, 6), (B1, 0, 2, 7), (B1, 0, 2, 3),
-    (B1, 0, 2, 6), (IM, 0, 0, 5), (IM, 0, 1, 2), (B3, 0, 2, 2), (B3, 0, 2, 5), (COL, 0, 1, 7), (COL, 0, 0, 7),
-    (TO, 0, 0, 2), (AC, 0, 1, 0), (AC, 0, 1, 1), (IM, 0, 1, 7), (AC, 0, 1, 2), (COL, 0, 2, 7), (TO, 0, 0, 1),
-    (AC, 0, 0, 5), (IM, 0, 1, 3), (B2, 0, 2, 1), (B3, 0, 2, 4), (IM, 0, 1, 5), (S1, 0, 0, 7), (B3, 0, 2, 0),
-    (S1, 0, 1, 6), (B2, 0, 2, 7), (IM, 0, 0, 6), (B2, 0, 2, 3), (S1, 0, 1, 4), (B2, 0, 2, 6), (IM, 0, 0, 7),
-    (AC, 0, 1, 3), (TO, 0, 1, 0), (S1, 0, 1, 7), (AC, 0, 0, 6), (TO, 0, 0, 3), (S1, 0, 1, 5), (TO, 0, 1, 2),
-    (TO, 0, 0, 4), (IM, 0, 1, 6), (B3, 0, 2, 1), (BF, 0, 2, 0), (AC, 0, 0, 7), (AC, 0, 1, 6), (B3, 0, 2, 7),
-    (B3, 0, 2, 3), (AC, 0, 1, 4), (B3, 0, 2, 6), (TO, 0, 1, 1), (AC, 0, 1, 7), (TO, 0, 0, 5), (TO, 0, 0, 6),
-    (AC, 0, 1, 5), (BI, 0, 2, 0), (BA, 0, 2, 0), (BO, 0, 2, 0), (TO, 0, 1, 4), (BI, 0, 2, 1), (BA, 0, 2, 1),
-    (TO, 0, 1, 3), (FIN, 0, 0, 0), (AGS, 1, 0, 0), (TO, 0, 1, 6), (TO, 0, 1, 5), (FIN, 0, 2, 0), (AGS, 1, 2, 0),
-    (FWD, 1, 0, 0), (WORK, 1, 0, 0), (COL, 1, 0, 0), (S1, 1, 0, 0), (COL, 1, 0, 1), (S1, 1, 0, 1), (FWD, 1, 2, 0),
-    (S1, 1, 0, 2), (FIN, 0, 1, 0), (AGS, 1, 1, 0), (COL, 1, 0, 2), (IM, 1, 0, 3), (IM, 1, 0, 1), (IM, 1, 0, 2),
-    (S1, 1, 0, 3), (IM, 1, 0, 0), (WORK, 1, 2, 0), (COL, 1, 2, 0), (B0, 1, 2, 0), (COL, 1, 2, 1), (AC, 1, 0, 0),
-    (B1, 1, 2, 5), (B0, 1, 2, 1), (B0, 1, 2, 2), (COL, 1, 2, 2), (FWD, 1, 1, 0), (AC, 1, 0, 2), (B1, 1, 2, 4),
-    (B1, 1, 2, 2), (AC, 1, 0, 1), (S1, 1, 0, 4), (IM, 1, 0, 4), (B1, 1, 2, 3), (B0, 1, 2, 3), (WORK, 1, 1, 0),
-    (COL, 1, 1, 0), (IM, 1, 1, 0), (B1, 1, 2, 0), (S1, 1, 1, 0), (COL, 1, 1, 1), (S1, 1, 1, 1), (S1, 1, 1, 2),
-    (AC, 1, 0, 3), (B2, 1, 2, 5), (COL, 1, 1, 2), (IM, 1, 1, 4), (TO, 1, 0, 0), (IM, 1, 1, 1), (IM, 1, 1, 3),
-    (B1, 1, 2, 1), (S1, 1, 1, 4), (B1, 1, 2, 6), (B2, 1, 2, 2), (IM, 1, 1, 2), (TO, 1, 0, 2), (S1, 1, 1, 3),
-    (B2, 1, 2, 4), (B2, 1, 2, 3), (AC, 1, 0, 4), (COL, 1, 0, 3), (AC, 1, 1, 0), (B2, 1, 2, 0), (S1, 1, 0, 6),
-    (S1, 1, 0, 5), (AC, 1, 1, 2), (COL, 1, 2, 3), (AC, 1, 1, 1), (TO, 1, 0, 1), (S1, 1, 0, 7), (B3, 1, 2, 5),
-    (COL, 1, 1, 3), (IM, 1, 1, 7), (IM, 1, 0, 6), (B3, 1, 2, 2), (S1, 1, 1, 6), (IM, 1, 1, 5), (AC, 1, 1, 4),
-    (B2, 1, 2, 6), (B1, 1, 2, 7), (B2, 1, 2, 1), (TO, 1, 0, 4), (IM, 1, 0, 5), (AC, 1, 1, 3), (B3, 1, 2, 3),
-    (B3, 1, 2, 4), (S1, 1, 1, 7), (TO, 1, 1, 0), (IM, 1, 0, 7), (IM, 1, 1, 6), (TO, 1, 1, 2), (B3, 1, 2, 0),
-    (AC, 1, 0, 6), (AC, 1, 0, 5), (TO, 1, 0, 3), (B3, 1, 2, 6), (AC, 1, 1, 6), (S1, 1, 1, 5), (AC, 1, 0, 7),
-    (B2, 1, 2, 7), (B3, 1, 2, 1), (AC, 1, 1, 7), (TO, 1, 1, 1), (TO, 1, 1, 4), (BF, 1, 2, 0), (TO, 1, 0, 6),
-    (BI, 1, 2, 1), (TO, 1, 0, 5), (AC, 1, 1, 5), (B3, 1, 2, 7), (BI, 1, 2, 0), (TO, 1, 1, 6), (TO, 1, 1, 3),
-    (BA, 1, 2, 1), (BA, 1, 2, 0), (FIN, 1, 0, 0), (AGS, 2, 0, 0), (BO, 1, 2, 0), (TO, 1, 1, 5), (FIN, 1, 2, 0),
-    (AGS, 2, 2, 0), (FWD, 2, 0, 0), (FIN, 1, 1, 0), (AGS, 2, 1, 0), (WORK, 2, 0, 0), (COL, 2, 0, 0), (S1, 2, 0, 0),
-    (FWD, 2, 2, 0), (COL, 2, 0, 1), (S1, 2, 0, 1), (S1, 2, 0, 2), (COL, 2, 0, 2), (WORK, 2, 2, 0), (COL, 2, 2, 0),
-    (B0, 2, 2, 0), (COL, 2, 2, 1), (FWD, 2, 1, 0), (B1, 2, 2, 5), (B0, 2, 2, 1), (IM, 2, 0, 3), (IM, 2, 0, 1),
-    (B0, 2, 2, 2), (IM, 2, 0, 2), (B1, 2, 2, 4), (COL, 2, 2, 2), (AC, 2, 0, 0), (B1, 2, 2, 2), (S1, 2, 0, 3),
-    (IM, 2, 0, 0), (B1, 2, 2, 3), (B0, 2, 2, 3), (S1, 2, 0, 4), (WORK, 2, 1, 0), (COL, 2, 1, 0), (S1, 2, 1, 0),
-    (COL, 2, 1, 1), (S1, 2, 1, 1), (IM, 2, 1, 0), (COL, 2, 1, 2), (B1, 2, 2, 0), (IM, 2, 1, 4), (S1, 2, 1, 2),
-    (S1, 2, 1, 3), (B2, 2, 2, 5), (AC, 2, 0, 2), (B1, 2, 2, 1), (IM, 2, 1, 2), (B1, 2, 2, 6), (S1, 2, 1, 4),
-    (B2, 2, 2, 2), (AC, 2, 0, 1), (COL, 2, 1, 3), (B2, 2, 2, 3), (IM, 2, 1, 7), (TO, 2, 0, 0), (COL, 2, 0, 3),
-    (AC, 2, 1, 0), (AC, 2, 1, 1), (B2, 2, 2, 0), (AC, 2, 0, 4), (S1, 2, 0, 6), (AC, 2, 0, 3), (B2, 2, 2, 4),
-    (COL, 2, 2, 3), (AC, 2, 1, 3), (AC, 2, 1, 2), (B3, 2, 2, 5), (IM, 2, 1, 1), (B2, 2, 2, 6), (B3, 2, 2, 2),
-    (S1, 2, 0, 5), (B1, 2, 2, 7), (B2, 2, 2, 1), (IM, 2, 0, 5), (B3, 2, 2, 3), (TO, 2, 0, 2), (S1, 2, 0, 7),
-    (IM, 2, 0, 7), (TO, 2, 1, 0), (S1, 2, 1, 5), (B3, 2, 2, 4), (TO, 2, 0, 1), (S1, 2, 1, 6), (IM, 2, 0, 6),
-    (IM, 2, 1, 3), (B3, 2, 2, 0), (IM, 2, 0, 4), (AC, 2, 0, 6), (TO, 2, 1, 2), (B3, 2, 2, 6), (S1, 2, 1, 7),
-    (AC, 2, 1, 4), (B3, 2, 2, 1), (B2, 2, 2, 7), (AC, 2, 0, 5), (IM, 2, 1, 5), (AC, 2, 0, 7), (TO, 2, 1, 1),
-    (AC, 2, 1, 5), (AC, 2, 1, 6), (TO, 2, 0, 3), (IM, 2, 1, 6), (BF, 2, 2, 0), (TO, 2, 0, 4), (BI, 2, 2, 1),
-    (AC, 2, 1, 7), (BI, 2, 2, 0), (TO, 2, 1, 4), (B3, 2, 2, 7), (TO, 2, 1, 3), (TO, 2, 0, 5), (BA, 2, 2, 1),
-    (TO, 2, 0, 6), (TO, 2, 1, 6), (TO, 2, 1, 5), (BA, 2, 2, 0), (BO, 2, 2, 0), (FIN, 2, 0, 0), (FIN, 2, 2, 0),
-    (FIN, 2, 1, 0),
+    (AGS, 0, 1, 0), (AGS, 0, 2, 0), (AGS, 0, 0, 0), (FWD, 0, 1, 0), (FWD, 0, 2, 0), (WORK, 0, 1, 0), (COL, 0, 1, 0),
+    (S1, 0, 1, 0), (IM, 0, 1, 0), (COL, 0, 1, 1), (S1, 0, 1, 1), (FWD, 0, 0, 0), (WORK, 0, 2, 0), (COL, 0, 2, 0),
+    (B0, 0, 2, 0), (B0, 0, 2, 1), (B0, 0, 2, 2), (B0, 0, 2, 3), (IM, 0, 1, 1), (COL, 0, 2, 1), (B1, 0, 2, 3),
+    (B1, 0, 2, 2), (WORK, 0, 0, 0), (COL, 0, 0, 0), (S1, 0, 0, 0), (COL, 0, 0, 1), (COL, 0, 1, 2), (COL, 0, 2, 2),
+    (AC, 0, 1, 0), (B1, 0, 2, 4), (IM, 0, 1, 2), (S1, 0, 1, 2), (COL, 0, 0, 2), (S1, 0, 0, 2), (S1, 0, 0, 1),
+    (IM, 0, 0, 1), (IM, 0, 0, 2), (B1, 0, 2, 5), (IM, 0, 0, 0), (AC, 0, 1, 1), (B1, 0, 2, 0), (B1, 0, 2, 6),
+    (COL, 0, 1, 3), (B1, 0, 2, 1), (S1, 0, 1, 3), (COL, 0, 2, 3), (AC, 0, 0, 0), (IM, 0, 1, 3), (B1, 0, 2, 7),
+    (COL, 0, 0, 3), (B2, 0, 2, 3), (S1, 0, 0, 3), (IM, 0, 0, 3), (TO, 0, 1, 0), (AC, 0, 1, 2), (B2, 0, 2, 2),
+    (AC, 0, 0, 2), (COL, 0, 1, 4), (COL, 0, 2, 4), (S1, 0, 1, 4), (B2, 0, 2, 0), (B2, 0, 2, 4), (IM, 0, 1, 4),
+    (COL, 0, 0, 4), (B2, 0, 2, 6), (B2, 0, 2, 5), (S1, 0, 0, 4), (IM, 0, 0, 4), (AC, 0, 0, 1), (B2, 0, 2, 1),
+    (B2, 0, 2, 7), (COL, 0, 1, 5), (S1, 0, 1, 5), (COL, 0, 2, 5), (TO, 0, 1, 1), (AC, 0, 1, 3), (B3, 0, 2, 3),
+    (IM, 0, 1, 5), (COL, 0, 0, 5), (TO, 0, 1, 2), (TO, 0, 0, 0), (S1, 0, 0, 5), (IM, 0, 0, 5), (TO, 0, 0, 2),
+    (B3, 0, 2, 2), (AC, 0, 0, 3), (COL, 0, 2, 6), (COL, 0, 1, 6), (AC, 0, 1, 4), (S1, 0, 1, 6), (COL, 0, 0, 6),
+    (B3, 0, 2, 4), (IM, 0, 1, 6), (S1, 0, 0, 6), (B3, 0, 2, 5), (AC, 0, 0, 4), (B3, 0, 2, 6), (B3, 0, 2, 0),
+    (B3, 0, 2, 1), (IM, 0, 0, 6), (B3, 0, 2, 7), (AC, 0, 1, 5), (COL, 0, 2, 7), (COL, 0, 1, 7), (S1, 0, 1, 7),
+    (COL, 0, 0, 7), (TO, 0, 0, 1), (TO, 0, 1, 3), (S1, 0, 0, 7), (IM, 0, 1, 7), (IM, 0, 0, 7), (AC, 0, 0, 5),
+    (TO, 0, 1, 4), (AC, 0, 1, 6), (BF, 0, 2, 0), (AC, 0, 0, 6), (BI, 0, 2, 0), (TO, 0, 0, 4), (BI, 0, 2, 1),
+    (TO, 0, 0, 3), (BO, 0, 2, 0), (TO, 0, 1, 5), (AC, 0, 1, 7), (AC, 0, 0, 7), (TO, 0, 1, 6), (BA, 0, 2, 1),
+    (BA, 0, 2, 0), (TO, 0, 0, 6), (TO, 0, 0, 5), (FIN, 0, 1, 0), (AGS, 1, 1, 0), (FIN, 0, 2, 0), (AGS, 1, 2, 0),
+    (FIN, 0, 0, 0), (AGS, 1, 0, 0), (FWD, 1, 1, 0), (FWD, 1, 2, 0), (WORK, 1, 1, 0), (COL, 1, 1, 0), (S1, 1, 1, 0),
+    (IM, 1, 1, 0), (COL, 1, 1, 1), (WORK, 1, 2, 0), (COL, 1, 2, 0), (B0, 1, 2, 0), (FWD, 1, 0, 0), (S1, 1, 1, 2),
+    (S1, 1, 1, 1), (COL, 1, 1, 2), (B0, 1, 2, 1), (B0, 1, 2, 2), (IM, 1, 1, 4), (IM, 1, 1, 2), (S1, 1, 1, 3),
+    (S1, 1, 1, 4), (B0, 1, 2, 3), (IM, 1, 1, 3), (IM, 1, 1, 1), (COL, 1, 2, 1), (B1, 1, 2, 2), (WORK, 1, 0, 0),
+    (COL, 1, 0, 0), (AC, 1, 1, 0), (S1, 1, 0, 0), (B1, 1, 2, 4), (B1, 1, 2, 3), (COL, 1, 0, 1), (S1, 1, 0, 2),
+    (S1, 1, 0, 1), (IM, 1, 0, 0), (COL, 1, 2, 2), (B1, 1, 2, 0), (AC, 1, 1, 2), (AC, 1, 1, 1), (B1, 1, 2, 5),
+    (COL, 1, 0, 2), (B1, 1, 2, 1), (B1, 1, 2, 6), (S1, 1, 0, 3), (AC, 1, 1, 4), (IM, 1, 0, 2), (S1, 1, 0, 4),
+    (IM, 1, 0, 3), (B1, 1, 2, 7), (B2, 1, 2, 2), (IM, 1, 0, 1), (IM, 1, 0, 4), (B2, 1, 2, 4), (B2, 1, 2, 3),
+    (AC, 1, 1, 3), (AC, 1, 0, 2), (TO, 1, 1, 0), (B2, 1, 2, 0), (B2, 1, 2, 5), (AC, 1, 0, 0), (B2, 1, 2, 1),
+    (TO, 1, 1, 2), (AC, 1, 0, 1), (B2, 1, 2, 6), (COL, 1, 0, 3), (COL, 1, 1, 3), (TO, 1, 1, 1), (S1, 1, 0, 6),
+    (S1, 1, 1, 6), (S1, 1, 1, 5), (COL, 1, 2, 3), (TO, 1, 1, 4), (S1, 1, 0, 7), (B3, 1, 2, 4), (AC, 1, 0, 4),
+    (B3, 1, 2, 0), (TO, 1, 0, 2), (AC, 1, 0, 3), (S1, 1, 0, 5), (IM, 1, 1, 5), (IM, 1, 1, 6), (S1, 1, 1, 7),
+    (IM, 1, 0, 7), (TO, 1, 0, 0), (B2, 1, 2, 7), (B3, 1, 2, 2), (IM, 1, 1, 7), (B3, 1, 2, 3), (IM, 1, 0, 5),
+    (B3, 1, 2, 6), (B3, 1, 2, 1), (IM, 1, 0, 6), (B3, 1, 2, 5), (AC, 1, 0, 6), (TO, 1, 1, 3), (AC, 1, 1, 5),
+    (AC, 1, 1, 6), (AC, 1, 0, 7), (TO, 1, 0, 1), (BF, 1, 2, 0), (AC, 1, 0, 5), (TO, 1, 0, 4), (B3, 1, 2, 7),
+    (AC, 1, 1, 7), (BI, 1, 2, 1), (BI, 1, 2, 0), (TO, 1, 1, 5), (TO, 1, 1, 6), (TO, 1, 0, 6), (TO, 1, 0, 3),
+    (BA, 1, 2, 1), (BA, 1, 2, 0), (BO, 1, 2, 0), (FIN, 1, 1, 0), (AGS, 2, 1, 0), (FIN, 1, 2, 0), (AGS, 2, 2, 0),
+    (TO, 1, 0, 5), (FWD, 2, 1, 0), (FIN, 1, 0, 0), (AGS, 2, 0, 0), (FWD, 2, 2, 0), (WORK, 2, 1, 0), (COL, 2, 1, 0),
+    (S1, 2, 1, 0), (IM, 2, 1, 0), (COL, 2, 1, 1), (S1, 2, 1, 1), (WORK, 2, 2, 0), (COL, 2, 2, 0), (B0, 2, 2, 0),
+    (S1, 2, 1, 2), (COL, 2, 1, 2), (FWD, 2, 0, 0), (B0, 2, 2, 2), (B0, 2, 2, 1), (B0, 2, 2, 3), (S1, 2, 1, 3),
+    (S1, 2, 1, 4), (IM, 2, 1, 2), (COL, 2, 2, 1), (B1, 2, 2, 2), (B1, 2, 2, 4), (B1, 2, 2, 3), (COL, 2, 2, 2),
+    (WORK, 2, 0, 0), (COL, 2, 0, 0), (S1, 2, 0, 0), (AC, 2, 1, 0), (COL, 2, 0, 1), (B1, 2, 2, 0), (AC, 2, 1, 2),
+    (S1, 2, 0, 1), (IM, 2, 0, 0), (S1, 2, 0, 2), (AC, 2, 1, 1), (B1, 2, 2, 5), (IM, 2, 0, 1), (COL, 2, 0, 2),
+    (B1, 2, 2, 1), (S1, 2, 0, 3), (S1, 2, 0, 4), (IM, 2, 0, 2), (AC, 2, 1, 3), (AC, 2, 1, 4), (B1, 2, 2, 6),
+    (B1, 2, 2, 7), (B2, 2, 2, 2), (IM, 2, 0, 3), (IM, 2, 0, 4), (B2, 2, 2, 4), (B2, 2, 2, 3), (IM, 2, 1, 1),
+    (AC, 2, 0, 0), (COL, 2, 2, 3), (TO, 2, 1, 0), (B2, 2, 2, 0), (AC, 2, 0, 1), (COL, 2, 1, 3), (B2, 2, 2, 1),
+    (AC, 2, 0, 2), (S1, 2, 1, 6), (COL, 2, 0, 3), (S1, 2, 0, 5), (TO, 2, 1, 2), (IM, 2, 1, 3), (IM, 2, 1, 4),
+    (S1, 2, 1, 5), (B2, 2, 2, 6), (B2, 2, 2, 5), (AC, 2, 0, 3), (B3, 2, 2, 4), (S1, 2, 0, 6), (IM, 2, 0, 5),
+    (B3, 2, 2, 3), (B3, 2, 2, 2), (IM, 2, 0, 6), (IM, 2, 1, 7), (S1, 2, 0, 7), (B2, 2, 2, 7), (IM, 2, 0, 7),
+    (IM, 2, 1, 6), (TO, 2, 0, 0), (B3, 2, 2, 0), (TO, 2, 1, 1), (IM, 2, 1, 5), (TO, 2, 0, 2), (S1, 2, 1, 7),
+    (B3, 2, 2, 1), (AC, 2, 0, 4), (AC, 2, 0, 5), (AC, 2, 1, 6), (TO, 2, 1, 4), (B3, 2, 2, 6), (AC, 2, 1, 5),
+    (AC, 2, 0, 6), (TO, 2, 0, 1), (B3, 2, 2, 5), (BF, 2, 2, 0), (AC, 2, 0, 7), (TO, 2, 1, 3), (B3, 2, 2, 7),
+    (AC, 2, 1, 7), (TO, 2, 0, 3), (TO, 2, 0, 4), (BI, 2, 2, 1), (TO, 2, 1, 6), (TO, 2, 1, 5), (BI, 2, 2, 0),
+    (BA, 2, 2, 0), (BA, 2, 2, 1), (BO, 2, 2, 0), (TO, 2, 0, 5), (TO, 2, 0, 6), (FIN, 2, 1, 0), (FIN, 2, 2, 0),
+    (FIN, 2, 0, 0),
 )
 
 
@@ -85,10 +86,10 @@
     slabs = (HALF, 4, 128)
     res = dict(
         pack=V(slabs, bf16), inb=V(slabs, bf16), outb=V(slabs, bf16),
-        meta=V((16, 128), i32), biasv=V((layers, 4, 1, 128), f32),
+        meta=V((8, 128), i32), cmeta=V((4, 128), i32), biasv=V((layers, 4, 1, 128), f32),
         wbuf=V((layers, 4, NZ, NXC, 128, 128), bf16),
-        metav=V((4, 8, 128), i32), colv=V((NXC * NZ, 8, 128), i32),
-        metas=pltpu.SMEM((4, 8, 128), i32), cols=pltpu.SMEM((NXC * NZ, 8, 128), i32),
+        metav=V((4, 8, 128), i32), colv=V((NXC * NZ, 4, 128), i32),
+        metas=pltpu.SMEM((4, 8, 128), i32), cols=pltpu.SMEM((NXC * NZ, 4, 128), i32),
         wl_sem=DMA((layers, NZ)), ws_sem=DMA((layers,)), wr_sem=DMA((layers, NZ)),
         ms_sem=DMA((3,)), mr_sem=DMA((3,)), cs_sem=DMA, cr_sem=DMA, loc_sem=DMA((2,)),
         in_s=DMA, in_r=DMA, out_s=DMA, out_r=DMA,
@@ -117,7 +118,7 @@
     f32, bf16 = jnp.float32, jnp.bfloat16
     s = dict(zip(scratch(LAYERS), refs))
     pack, inb, outb, meta, biasv, wbuf = (s[n] for n in ("pack", "inb", "outb", "meta", "biasv", "wbuf"))
-    metav, colv, metas, cols = (s[n] for n in ("metav", "colv", "metas", "cols"))
+    metav, colv, metas, cols, cmeta = (s[n] for n in ("metav", "colv", "metas", "cols", "cmeta"))
     nx, ny, im = lax.axis_index("nx"), lax.axis_index("ny"), lax.axis_index("img")
     x, c = nx // 2, nx % 2
     yl, z = ny // NZ, ny % NZ
@@ -147,17 +148,18 @@
         far = 4 - (k + 1) // 2
         return (z + NZ + jnp.where(k % 2 == 1, far, -far)) % NZ
 
+    spread = (4, 12, 3, 13, 5, 11, 2, 14, 6, 10, 1, 15, 7, 9, 8)
+
     def for_half(fn):
-        for b in range(1, NY):
-            fn(nx * NY + (ny + b) % NY, (nx, (ny + b) % NY, im))
-
-        def rows(a, carry):
-            n = (nx + a) % (2 * NXC)
-            for b in range(NY):
+        def rows(t, carry):
+            n = (nx + 4 + (t + 1) // 2 * (1 - 2 * (t % 2))) % (2 * NXC)
+            for b in spread + (0,):
                 fn(n * NY + (ny + b) % NY, (n, (ny + b) % NY, im))
             return carry
 
-        lax.fori_loop(1, 2 * NXC, rows, 0)
+        lax.fori_loop(0, 2 * NXC - 1, rows, 0)
+        for b in spread:
+            fn(nx * NY + (ny + b) % NY, (nx, (ny + b) % NY, im))
 
     def for_plane(fn):
         def step(j, carry):
@@ -183,25 +185,27 @@
     for i in range(layers):
         meta[i, :] = row_in[i, 0, :]
         meta[3 + i, :] = live_in[i, 0, :]
-        meta[8 + i, :] = col_in[i, 0, :]
+        cmeta[i, :] = col_in[i, 0, :]
         for r in range(4):
             biasv[i, r, 0, :] = bias[i, r * 128:(r + 1) * 128]
-    metav[me] = meta[pl.ds(0, 8), :]
-    colv[plane] = meta[pl.ds(8, 8), :]
+    cmeta[3, :] = cmeta[0, :]
+    meta[6, :] = meta[0, :]
+    meta[7, :] = meta[0, :]
+    metav[me] = meta[...]
+    colv[plane] = cmeta[...]
     pl.semaphore_wait(barrier, 2 + HALF - 1)
 
     for_half(lambda k, d: remote(pack.at[k], inb.at[flat], s["in_s"], s["in_r"], d).start())
 
     def meta_cp(k, d):
-        return remote(meta.at[pl.ds(0, 8)], metav.at[me], s["ms_sem"].at[k], s["mr_sem"].at[k], d)
+        return remote(meta, metav.at[me], s["ms_sem"].at[k], s["mr_sem"].at[k], d)
 
     group = ((0, partner, yl * 2 + 1 - c), (1, near, (1 - yl) * 2 + c), (2, diag, (1 - yl) * 2 + 1 - c))
     for k, d, _ in group:
         meta_cp(k, d).start()
-    for_plane(lambda j, d: remote(meta.at[pl.ds(8, 8)], colv.at[plane], s["cs_sem"], s["cr_sem"], d).start())
 
     def start_weights(l, lo, hi):
-        def step(k, carry):
+        def column_copies(k, both):
             zz = col_z(k)
 
             def send(x0, n, cc, yy, ii):
@@ -209,13 +213,26 @@
                        s["ws_sem"].at[l], s["wr_sem"].at[l, k], dev(x, cc, yy, z, ii)).start()
 
             for cc in (0, 1):
-                send(0, 2, cc, 1 - yl, im_up)
-                send(2, 2, cc, 1 - yl, im_dn)
+                if both:
+                    send(0, 2, cc, 1 - yl, im_up)
+                    send(2, 2, cc, 1 - yl, im_dn)
+                else:
+                    send(0, 4, cc, 1 - yl, 1 - im)
             send(0, 4, 1 - c, yl, im)
             pltpu.make_async_copy(w_hbm.at[l, :, c, yl, zz], wbuf.at[l, me, k], s["wl_sem"].at[l, k]).start()
-            return carry
-
-        lax.fori_loop(lo, hi, step, 0)
+
+        def step(both):
+            def run(k, carry):
+                column_copies(k, both)
+                return carry
+
+            return run
+
+        split = SPLIT if l else NZ
+        if lo < split:
+            lax.fori_loop(lo, min(hi, split), step(True), 0)
+        if hi > split:
+            lax.fori_loop(max(lo, split), hi, step(False), 0)
 
     def wait_weights(l, k):
         pltpu.make_async_copy(w_hbm.at[l, :, c, yl, 0], wbuf.at[l, me, k], s["wl_sem"].at[l, k]).wait()
@@ -223,17 +240,7 @@
         remote(three, three, s["ws_sem"].at[l], s["wr_sem"].at[l, k], partner).wait_recv()
 
     start_weights(0, 0, FIRST)
-    for k, d, src in group:
-        remote(meta.at[pl.ds(0, 8)], metav.at[src], s["ms_sem"].at[k], s["mr_sem"].at[k], d).wait_recv()
-        meta_cp(k, d).wait_send()
-    lot = colv.at[pl.ds(0, NXC * NZ - 1)]
-    lot = remote(lot, lot, s["cs_sem"], s["cr_sem"], partner)
-    lot.wait_recv()
-    lot.wait_send()
-    tables = (pltpu.make_async_copy(metav, metas, s["loc_sem"].at[0]),
-              pltpu.make_async_copy(colv, cols, s["loc_sem"].at[1]))
-    for cp in tables:
-        cp.start()
+    for_plane(lambda j, d: remote(cmeta, colv.at[plane], s["cs_sem"], s["cr_sem"], d).start())
     inb[flat] = pack[flat]
     lot = remote(pack.at[pl.ds(0, HALF - 1)], inb.at[pl.ds(0, HALF - 1)], s["in_s"], s["in_r"], partner)
     lot.wait_recv()
@@ -241,6 +248,20 @@
         rows = inb[:, r, :]
         for i, (_, m) in enumerate(STREAMS):
             s[f"act{i}"][0, me, r] = rows[OFFSET[i]:OFFSET[i] + m]
+
+    tables = (pltpu.make_async_copy(metav, metas, s["loc_sem"].at[0]),
+              pltpu.make_async_copy(colv, cols, s["loc_sem"].at[1]))
+
+    def take_tables():
+        for k, d, src in group:
+            remote(meta, metav.at[src], s["ms_sem"].at[k], s["mr_sem"].at[k], d).wait_recv()
+            meta_cp(k, d).wait_send()
+        most = colv.at[pl.ds(0, NXC * NZ - 1)]
+        most = remote(most, most, s["cs_sem"], s["cr_sem"], partner)
+        most.wait_recv()
+        most.wait_send()
+        for cp in tables:
+            cp.start()
 
     def ag(l, i, src, slot, d):
         ref = s[f"act{i}"].at[l, src]
@@ -414,13 +435,14 @@
             for cp in tables:
                 cp.wait()
         steps[name](l, i, arg)
-        if name in (AGS, FWD):
+        if name == AGS and l == 0 or name == FWD:
             count[name, l] = count.get((name, l), 0) + 1
             if count[name, l] == len(STREAMS):
                 if name == AGS:
-                    start_weights(l, EARLY if l else FIRST, NZ)
+                    start_weights(0, FIRST, NZ)
+                    take_tables()
                 elif l < layers - 1:
-                    start_weights(l + 1, 0, EARLY)
+                    start_weights(l + 1, 0, NZ)
 
     for r in range(4):
         for i, (_, m) in enumerate(STREAMS):

time: 140 us -> 135 us (0.964)
  Pallas kernels: 138 us -> 134 us
    pallas_call x1, Pallas kernels: 138 us -> 134 us  [run_layers(): pl.pallas_call(layers_kernel, out_shape=jax.ShapeDtypeStruct((HALF, 4, 12...]
where the time goes in v6:
time: 135 us
  Pallas kernels  134 us (99%)
  local copies, waits for them, and re-layouts  1.66 us (1%)
    pallas_call x1, Pallas kernels, run_layers(): pl.pallas_call(layers_kernel, out_shape=jax.ShapeDtypeStruct((HALF, 4, 12...  134 us

profile of v6, /device:TPU:1, one launch (start us, length us, event | category | flops | bytes accessed | tf_op | source)
XLA Modules:
  0.0 135.3 jit_solution(8305360025259584795)
XLA Ops:
  0.0 133.7 %shard_map.64 = bf16[128,4,128]{2,1,0:T(4,128)(2,1)} custom-call(bf16[3,4,2,2,8,128,128]{6,5,4,3,2,1,0:T(8,128)(2,1)} %bitcast.3, bf16[128,4,1,128]{3,2,1,0:T(2,128)(2,1)} %bitcast.4, s32[3,1,128]{2,1,0:T(1,128)} %row_in.1, s32[3,1,128]{2,1,0:T(1,128)} %live_in.1, s32[3,1,128]{2,1,0:T(1,128)} %bitcast.5, f32[3,512]{1,0:T(4,128)} %bias.1), custom_call_target="tpu_custom_call" | custom-call | tf_op jit(solution)/shard_map/pallas_call | solution.py:465
  133.7 1.7 %reshape.11 = bf16[1,65536]{1,0:T(2,128)(2,1)} reshape(bf16[128,4,128]{2,1,0:T(4,128)(2,1)} %shard_map.64) | data formatting | bytes 262144 | tf_op jit(solution)/shard_map/reshape | solution.py:480

commit v7 on v6

--- a/solution.py
+++ b/solution.py
@@ -20,59 +20,59 @@
 SEGS = (((0,), (1,), (2,), (3,), (4,), (5,), (6,), (7,)), ((0,), (1, 2), (3, 4), (5, 6, 7)))
 AGS, FWD, WORK, COL, S1, IM, AC, TO, FIN, B0, B1, B2, B3, BF, BI, BA, BO = range(17)
 ORDER = (
-    (AGS, 0, 1, 0), (AGS, 0, 2, 0), (AGS, 0, 0, 0), (FWD, 0, 1, 0), (FWD, 0, 2, 0), (WORK, 0, 1, 0), (COL, 0, 1, 0),
-    (S1, 0, 1, 0), (IM, 0, 1, 0), (COL, 0, 1, 1), (S1, 0, 1, 1), (FWD, 0, 0, 0), (WORK, 0, 2, 0), (COL, 0, 2, 0),
-    (B0, 0, 2, 0), (B0, 0, 2, 1), (B0, 0, 2, 2), (B0, 0, 2, 3), (IM, 0, 1, 1), (COL, 0, 2, 1), (B1, 0, 2, 3),
-    (B1, 0, 2, 2), (WORK, 0, 0, 0), (COL, 0, 0, 0), (S1, 0, 0, 0), (COL, 0, 0, 1), (COL, 0, 1, 2), (COL, 0, 2, 2),
-    (AC, 0, 1, 0), (B1, 0, 2, 4), (IM, 0, 1, 2), (S1, 0, 1, 2), (COL, 0, 0, 2), (S1, 0, 0, 2), (S1, 0, 0, 1),
-    (IM, 0, 0, 1), (IM, 0, 0, 2), (B1, 0, 2, 5), (IM, 0, 0, 0), (AC, 0, 1, 1), (B1, 0, 2, 0), (B1, 0, 2, 6),
-    (COL, 0, 1, 3), (B1, 0, 2, 1), (S1, 0, 1, 3), (COL, 0, 2, 3), (AC, 0, 0, 0), (IM, 0, 1, 3), (B1, 0, 2, 7),
-    (COL, 0, 0, 3), (B2, 0, 2, 3), (S1, 0, 0, 3), (IM, 0, 0, 3), (TO, 0, 1, 0), (AC, 0, 1, 2), (B2, 0, 2, 2),
-    (AC, 0, 0, 2), (COL, 0, 1, 4), (COL, 0, 2, 4), (S1, 0, 1, 4), (B2, 0, 2, 0), (B2, 0, 2, 4), (IM, 0, 1, 4),
-    (COL, 0, 0, 4), (B2, 0, 2, 6), (B2, 0, 2, 5), (S1, 0, 0, 4), (IM, 0, 0, 4), (AC, 0, 0, 1), (B2, 0, 2, 1),
-    (B2, 0, 2, 7), (COL, 0, 1, 5), (S1, 0, 1, 5), (COL, 0, 2, 5), (TO, 0, 1, 1), (AC, 0, 1, 3), (B3, 0, 2, 3),
-    (IM, 0, 1, 5), (COL, 0, 0, 5), (TO, 0, 1, 2), (TO, 0, 0, 0), (S1, 0, 0, 5), (IM, 0, 0, 5), (TO, 0, 0, 2),
-    (B3, 0, 2, 2), (AC, 0, 0, 3), (COL, 0, 2, 6), (COL, 0, 1, 6), (AC, 0, 1, 4), (S1, 0, 1, 6), (COL, 0, 0, 6),
-    (B3, 0, 2, 4), (IM, 0, 1, 6), (S1, 0, 0, 6), (B3, 0, 2, 5), (AC, 0, 0, 4), (B3, 0, 2, 6), (B3, 0, 2, 0),
-    (B3, 0, 2, 1), (IM, 0, 0, 6), (B3, 0, 2, 7), (AC, 0, 1, 5), (COL, 0, 2, 7), (COL, 0, 1, 7), (S1, 0, 1, 7),
-    (COL, 0, 0, 7), (TO, 0, 0, 1), (TO, 0, 1, 3), (S1, 0, 0, 7), (IM, 0, 1, 7), (IM, 0, 0, 7), (AC, 0, 0, 5),
-    (TO, 0, 1, 4), (AC, 0, 1, 6), (BF, 0, 2, 0), (AC, 0, 0, 6), (BI, 0, 2, 0), (TO, 0, 0, 4), (BI, 0, 2, 1),
-    (TO, 0, 0, 3), (BO, 0, 2, 0), (TO, 0, 1, 5), (AC, 0, 1, 7), (AC, 0, 0, 7), (TO, 0, 1, 6), (BA, 0, 2, 1),
-    (BA, 0, 2, 0), (TO, 0, 0, 6), (TO, 0, 0, 5), (FIN, 0, 1, 0), (AGS, 1, 1, 0), (FIN, 0, 2, 0), (AGS, 1, 2, 0),
-    (FIN, 0, 0, 0), (AGS, 1, 0, 0), (FWD, 1, 1, 0), (FWD, 1, 2, 0), (WORK, 1, 1, 0), (COL, 1, 1, 0), (S1, 1, 1, 0),
-    (IM, 1, 1, 0), (COL, 1, 1, 1), (WORK, 1, 2, 0), (COL, 1, 2, 0), (B0, 1, 2, 0), (FWD, 1, 0, 0), (S1, 1, 1, 2),
-    (S1, 1, 1, 1), (COL, 1, 1, 2), (B0, 1, 2, 1), (B0, 1, 2, 2), (IM, 1, 1, 4), (IM, 1, 1, 2), (S1, 1, 1, 3),
-    (S1, 1, 1, 4), (B0, 1, 2, 3), (IM, 1, 1, 3), (IM, 1, 1, 1), (COL, 1, 2, 1), (B1, 1, 2, 2), (WORK, 1, 0, 0),
-    (COL, 1, 0, 0), (AC, 1, 1, 0), (S1, 1, 0, 0), (B1, 1, 2, 4), (B1, 1, 2, 3), (COL, 1, 0, 1), (S1, 1, 0, 2),
-    (S1, 1, 0, 1), (IM, 1, 0, 0), (COL, 1, 2, 2), (B1, 1, 2, 0), (AC, 1, 1, 2), (AC, 1, 1, 1), (B1, 1, 2, 5),
-    (COL, 1, 0, 2), (B1, 1, 2, 1), (B1, 1, 2, 6), (S1, 1, 0, 3), (AC, 1, 1, 4), (IM, 1, 0, 2), (S1, 1, 0, 4),
-    (IM, 1, 0, 3), (B1, 1, 2, 7), (B2, 1, 2, 2), (IM, 1, 0, 1), (IM, 1, 0, 4), (B2, 1, 2, 4), (B2, 1, 2, 3),
-    (AC, 1, 1, 3), (AC, 1, 0, 2), (TO, 1, 1, 0), (B2, 1, 2, 0), (B2, 1, 2, 5), (AC, 1, 0, 0), (B2, 1, 2, 1),
-    (TO, 1, 1, 2), (AC, 1, 0, 1), (B2, 1, 2, 6), (COL, 1, 0, 3), (COL, 1, 1, 3), (TO, 1, 1, 1), (S1, 1, 0, 6),
-    (S1, 1, 1, 6), (S1, 1, 1, 5), (COL, 1, 2, 3), (TO, 1, 1, 4), (S1, 1, 0, 7), (B3, 1, 2, 4), (AC, 1, 0, 4),
-    (B3, 1, 2, 0), (TO, 1, 0, 2), (AC, 1, 0, 3), (S1, 1, 0, 5), (IM, 1, 1, 5), (IM, 1, 1, 6), (S1, 1, 1, 7),
-    (IM, 1, 0, 7), (TO, 1, 0, 0), (B2, 1, 2, 7), (B3, 1, 2, 2), (IM, 1, 1, 7), (B3, 1, 2, 3), (IM, 1, 0, 5),
-    (B3, 1, 2, 6), (B3, 1, 2, 1), (IM, 1, 0, 6), (B3, 1, 2, 5), (AC, 1, 0, 6), (TO, 1, 1, 3), (AC, 1, 1, 5),
-    (AC, 1, 1, 6), (AC, 1, 0, 7), (TO, 1, 0, 1), (BF, 1, 2, 0), (AC, 1, 0, 5), (TO, 1, 0, 4), (B3, 1, 2, 7),
-    (AC, 1, 1, 7), (BI, 1, 2, 1), (BI, 1, 2, 0), (TO, 1, 1, 5), (TO, 1, 1, 6), (TO, 1, 0, 6), (TO, 1, 0, 3),
-    (BA, 1, 2, 1), (BA, 1, 2, 0), (BO, 1, 2, 0), (FIN, 1, 1, 0), (AGS, 2, 1, 0), (FIN, 1, 2, 0), (AGS, 2, 2, 0),
-    (TO, 1, 0, 5), (FWD, 2, 1, 0), (FIN, 1, 0, 0), (AGS, 2, 0, 0), (FWD, 2, 2, 0), (WORK, 2, 1, 0), (COL, 2, 1, 0),
-    (S1, 2, 1, 0), (IM, 2, 1, 0), (COL, 2, 1, 1), (S1, 2, 1, 1), (WORK, 2, 2, 0), (COL, 2, 2, 0), (B0, 2, 2, 0),
-    (S1, 2, 1, 2), (COL, 2, 1, 2), (FWD, 2, 0, 0), (B0, 2, 2, 2), (B0, 2, 2, 1), (B0, 2, 2, 3), (S1, 2, 1, 3),
-    (S1, 2, 1, 4), (IM, 2, 1, 2), (COL, 2, 2, 1), (B1, 2, 2, 2), (B1, 2, 2, 4), (B1, 2, 2, 3), (COL, 2, 2, 2),
-    (WORK, 2, 0, 0), (COL, 2, 0, 0), (S1, 2, 0, 0), (AC, 2, 1, 0), (COL, 2, 0, 1), (B1, 2, 2, 0), (AC, 2, 1, 2),
-    (S1, 2, 0, 1), (IM, 2, 0, 0), (S1, 2, 0, 2), (AC, 2, 1, 1), (B1, 2, 2, 5), (IM, 2, 0, 1), (COL, 2, 0, 2),
-    (B1, 2, 2, 1), (S1, 2, 0, 3), (S1, 2, 0, 4), (IM, 2, 0, 2), (AC, 2, 1, 3), (AC, 2, 1, 4), (B1, 2, 2, 6),
-    (B1, 2, 2, 7), (B2, 2, 2, 2), (IM, 2, 0, 3), (IM, 2, 0, 4), (B2, 2, 2, 4), (B2, 2, 2, 3), (IM, 2, 1, 1),
-    (AC, 2, 0, 0), (COL, 2, 2, 3), (TO, 2, 1, 0), (B2, 2, 2, 0), (AC, 2, 0, 1), (COL, 2, 1, 3), (B2, 2, 2, 1),
-    (AC, 2, 0, 2), (S1, 2, 1, 6), (COL, 2, 0, 3), (S1, 2, 0, 5), (TO, 2, 1, 2), (IM, 2, 1, 3), (IM, 2, 1, 4),
-    (S1, 2, 1, 5), (B2, 2, 2, 6), (B2, 2, 2, 5), (AC, 2, 0, 3), (B3, 2, 2, 4), (S1, 2, 0, 6), (IM, 2, 0, 5),
-    (B3, 2, 2, 3), (B3, 2, 2, 2), (IM, 2, 0, 6), (IM, 2, 1, 7), (S1, 2, 0, 7), (B2, 2, 2, 7), (IM, 2, 0, 7),
-    (IM, 2, 1, 6), (TO, 2, 0, 0), (B3, 2, 2, 0), (TO, 2, 1, 1), (IM, 2, 1, 5), (TO, 2, 0, 2), (S1, 2, 1, 7),
-    (B3, 2, 2, 1), (AC, 2, 0, 4), (AC, 2, 0, 5), (AC, 2, 1, 6), (TO, 2, 1, 4), (B3, 2, 2, 6), (AC, 2, 1, 5),
-    (AC, 2, 0, 6), (TO, 2, 0, 1), (B3, 2, 2, 5), (BF, 2, 2, 0), (AC, 2, 0, 7), (TO, 2, 1, 3), (B3, 2, 2, 7),
-    (AC, 2, 1, 7), (TO, 2, 0, 3), (TO, 2, 0, 4), (BI, 2, 2, 1), (TO, 2, 1, 6), (TO, 2, 1, 5), (BI, 2, 2, 0),
-    (BA, 2, 2, 0), (BA, 2, 2, 1), (BO, 2, 2, 0), (TO, 2, 0, 5), (TO, 2, 0, 6), (FIN, 2, 1, 0), (FIN, 2, 2, 0),
+    (AGS, 0, 2, 0), (AGS, 0, 1, 0), (AGS, 0, 0, 0), (FWD, 0, 2, 0), (FWD, 0, 1, 0), (WORK, 0, 2, 0), (COL, 0, 2, 0),
+    (B0, 0, 2, 0), (COL, 0, 2, 1), (B1, 0, 2, 3), (B1, 0, 2, 2), (FWD, 0, 0, 0), (B0, 0, 2, 2), (B0, 0, 2, 1),
+    (WORK, 0, 1, 0), (B0, 0, 2, 3), (COL, 0, 1, 0), (IM, 0, 1, 0), (S1, 0, 1, 0), (COL, 0, 1, 1), (S1, 0, 1, 1),
+    (IM, 0, 1, 1), (WORK, 0, 0, 0), (COL, 0, 0, 0), (IM, 0, 0, 0), (S1, 0, 0, 0), (COL, 0, 0, 1), (IM, 0, 0, 1),
+    (COL, 0, 0, 2), (S1, 0, 0, 2), (S1, 0, 0, 1), (COL, 0, 2, 2), (B1, 0, 2, 5), (IM, 0, 0, 2), (B1, 0, 2, 4),
+    (COL, 0, 1, 2), (B1, 0, 2, 6), (IM, 0, 1, 2), (S1, 0, 1, 2), (B1, 0, 2, 0), (AC, 0, 1, 0), (B1, 0, 2, 7),
+    (COL, 0, 2, 3), (AC, 0, 1, 1), (COL, 0, 0, 3), (S1, 0, 0, 3), (IM, 0, 0, 3), (B2, 0, 2, 2), (COL, 0, 1, 3),
+    (B1, 0, 2, 1), (IM, 0, 1, 3), (S1, 0, 1, 3), (AC, 0, 0, 0), (B2, 0, 2, 3), (AC, 0, 0, 1), (AC, 0, 0, 2),
+    (B2, 0, 2, 0), (COL, 0, 1, 4), (COL, 0, 2, 4), (B2, 0, 2, 5), (AC, 0, 1, 2), (IM, 0, 1, 4), (S1, 0, 1, 4),
+    (B2, 0, 2, 4), (COL, 0, 0, 4), (B2, 0, 2, 6), (S1, 0, 0, 4), (IM, 0, 0, 4), (TO, 0, 1, 0), (B2, 0, 2, 7),
+    (COL, 0, 0, 5), (COL, 0, 2, 5), (S1, 0, 0, 5), (B2, 0, 2, 1), (IM, 0, 0, 5), (B3, 0, 2, 2), (TO, 0, 0, 2),
+    (COL, 0, 1, 5), (S1, 0, 1, 5), (B3, 0, 2, 3), (AC, 0, 0, 3), (IM, 0, 1, 5), (AC, 0, 1, 3), (TO, 0, 1, 2),
+    (B3, 0, 2, 0), (TO, 0, 0, 0), (COL, 0, 1, 6), (S1, 0, 1, 6), (COL, 0, 2, 6), (AC, 0, 1, 4), (B3, 0, 2, 4),
+    (AC, 0, 0, 4), (B3, 0, 2, 5), (B3, 0, 2, 6), (IM, 0, 1, 6), (COL, 0, 0, 6), (IM, 0, 0, 6), (S1, 0, 0, 6),
+    (TO, 0, 1, 1), (B3, 0, 2, 1), (B3, 0, 2, 7), (AC, 0, 0, 5), (COL, 0, 0, 7), (IM, 0, 0, 7), (COL, 0, 1, 7),
+    (AC, 0, 1, 5), (IM, 0, 1, 7), (COL, 0, 2, 7), (AC, 0, 1, 6), (S1, 0, 1, 7), (S1, 0, 0, 7), (BF, 0, 2, 0),
+    (TO, 0, 1, 4), (TO, 0, 0, 1), (TO, 0, 0, 4), (AC, 0, 0, 6), (TO, 0, 1, 3), (BI, 0, 2, 1), (BI, 0, 2, 0),
+    (BO, 0, 2, 0), (TO, 0, 0, 3), (TO, 0, 1, 6), (BA, 0, 2, 1), (AC, 0, 1, 7), (TO, 0, 1, 5), (TO, 0, 0, 6),
+    (AC, 0, 0, 7), (BA, 0, 2, 0), (TO, 0, 0, 5), (FIN, 0, 1, 0), (AGS, 1, 1, 0), (FIN, 0, 2, 0), (AGS, 1, 2, 0),
+    (FIN, 0, 0, 0), (AGS, 1, 0, 0), (FWD, 1, 1, 0), (FWD, 1, 2, 0), (WORK, 1, 1, 0), (COL, 1, 1, 0), (IM, 1, 1, 0),
+    (S1, 1, 1, 0), (FWD, 1, 0, 0), (COL, 1, 1, 1), (S1, 1, 1, 2), (S1, 1, 1, 1), (WORK, 1, 2, 0), (COL, 1, 2, 0),
+    (B0, 1, 2, 0), (B0, 1, 2, 2), (B0, 1, 2, 3), (WORK, 1, 0, 0), (COL, 1, 0, 0), (S1, 1, 0, 0), (IM, 1, 0, 0),
+    (COL, 1, 0, 1), (S1, 1, 0, 2), (IM, 1, 0, 2), (COL, 1, 0, 2), (AC, 1, 1, 0), (S1, 1, 0, 4), (S1, 1, 0, 3),
+    (IM, 1, 0, 3), (IM, 1, 0, 1), (B0, 1, 2, 1), (COL, 1, 2, 1), (B1, 1, 2, 2), (AC, 1, 1, 1), (AC, 1, 1, 2),
+    (B1, 1, 2, 3), (B1, 1, 2, 4), (S1, 1, 0, 1), (IM, 1, 1, 1), (B1, 1, 2, 5), (IM, 1, 1, 2), (COL, 1, 2, 2),
+    (B1, 1, 2, 0), (B1, 1, 2, 6), (AC, 1, 0, 0), (IM, 1, 0, 4), (COL, 1, 1, 2), (S1, 1, 1, 3), (B1, 1, 2, 7),
+    (S1, 1, 1, 4), (IM, 1, 1, 4), (IM, 1, 1, 3), (AC, 1, 0, 2), (AC, 1, 0, 4), (TO, 1, 1, 0), (B1, 1, 2, 1),
+    (AC, 1, 0, 3), (B2, 1, 2, 2), (B2, 1, 2, 4), (B2, 1, 2, 3), (B2, 1, 2, 5), (AC, 1, 0, 1), (B2, 1, 2, 0),
+    (B2, 1, 2, 6), (TO, 1, 1, 2), (COL, 1, 0, 3), (AC, 1, 1, 4), (IM, 1, 0, 5), (B2, 1, 2, 7), (S1, 1, 0, 5),
+    (TO, 1, 1, 1), (TO, 1, 0, 0), (IM, 1, 0, 6), (IM, 1, 0, 7), (COL, 1, 2, 3), (B3, 1, 2, 4), (AC, 1, 1, 3),
+    (B3, 1, 2, 2), (B2, 1, 2, 1), (TO, 1, 0, 2), (S1, 1, 0, 6), (COL, 1, 1, 3), (S1, 1, 1, 6), (S1, 1, 1, 5),
+    (B3, 1, 2, 3), (IM, 1, 1, 7), (S1, 1, 1, 7), (B3, 1, 2, 6), (IM, 1, 1, 6), (B3, 1, 2, 5), (IM, 1, 1, 5),
+    (S1, 1, 0, 7), (B3, 1, 2, 0), (TO, 1, 1, 4), (AC, 1, 0, 5), (B3, 1, 2, 7), (TO, 1, 0, 1), (TO, 1, 1, 3),
+    (AC, 1, 0, 6), (TO, 1, 0, 4), (AC, 1, 1, 5), (AC, 1, 1, 6), (B3, 1, 2, 1), (BI, 1, 2, 1), (AC, 1, 1, 7),
+    (BF, 1, 2, 0), (AC, 1, 0, 7), (TO, 1, 0, 3), (BO, 1, 2, 0), (TO, 1, 1, 6), (TO, 1, 0, 6), (TO, 1, 1, 5),
+    (BI, 1, 2, 0), (BA, 1, 2, 1), (BA, 1, 2, 0), (TO, 1, 0, 5), (FIN, 1, 1, 0), (AGS, 2, 1, 0), (FIN, 1, 2, 0),
+    (AGS, 2, 2, 0), (FIN, 1, 0, 0), (AGS, 2, 0, 0), (FWD, 2, 1, 0), (FWD, 2, 2, 0), (WORK, 2, 1, 0), (COL, 2, 1, 0),
+    (IM, 2, 1, 0), (FWD, 2, 0, 0), (S1, 2, 1, 0), (COL, 2, 1, 1), (WORK, 2, 2, 0), (S1, 2, 1, 1), (IM, 2, 1, 1),
+    (COL, 2, 2, 0), (B0, 2, 2, 0), (B0, 2, 2, 1), (WORK, 2, 0, 0), (COL, 2, 0, 0), (IM, 2, 0, 0), (S1, 2, 0, 0),
+    (S1, 2, 1, 2), (B0, 2, 2, 3), (IM, 2, 1, 2), (B0, 2, 2, 2), (COL, 2, 0, 1), (S1, 2, 0, 2), (S1, 2, 0, 1),
+    (COL, 2, 2, 1), (B1, 2, 2, 3), (B1, 2, 2, 2), (B1, 2, 2, 4), (B1, 2, 2, 5), (AC, 2, 1, 0), (COL, 2, 0, 2),
+    (S1, 2, 0, 4), (S1, 2, 0, 3), (IM, 2, 0, 3), (COL, 2, 2, 2), (B1, 2, 2, 0), (B1, 2, 2, 7), (AC, 2, 0, 0),
+    (COL, 2, 1, 2), (IM, 2, 1, 4), (B1, 2, 2, 6), (S1, 2, 1, 3), (AC, 2, 1, 2), (S1, 2, 1, 4), (B1, 2, 2, 1),
+    (IM, 2, 1, 3), (IM, 2, 0, 1), (AC, 2, 1, 1), (AC, 2, 0, 1), (IM, 2, 0, 2), (AC, 2, 0, 2), (IM, 2, 0, 4),
+    (B2, 2, 2, 3), (B2, 2, 2, 4), (TO, 2, 1, 0), (AC, 2, 0, 4), (B2, 2, 2, 2), (AC, 2, 0, 3), (B2, 2, 2, 5),
+    (COL, 2, 0, 3), (IM, 2, 0, 6), (S1, 2, 0, 5), (IM, 2, 0, 7), (TO, 2, 0, 0), (B2, 2, 2, 7), (COL, 2, 2, 3),
+    (B3, 2, 2, 3), (AC, 2, 1, 4), (B2, 2, 2, 6), (S1, 2, 0, 6), (B2, 2, 2, 0), (B3, 2, 2, 4), (AC, 2, 1, 3),
+    (B2, 2, 2, 1), (COL, 2, 1, 3), (S1, 2, 1, 6), (S1, 2, 1, 5), (IM, 2, 1, 7), (B3, 2, 2, 5), (IM, 2, 1, 5),
+    (IM, 2, 1, 6), (TO, 2, 1, 2), (S1, 2, 0, 7), (TO, 2, 1, 1), (IM, 2, 0, 5), (B3, 2, 2, 2), (S1, 2, 1, 7),
+    (TO, 2, 0, 2), (B3, 2, 2, 7), (TO, 2, 0, 1), (B3, 2, 2, 6), (B3, 2, 2, 0), (AC, 2, 0, 5), (AC, 2, 0, 6),
+    (B3, 2, 2, 1), (AC, 2, 1, 6), (TO, 2, 1, 3), (TO, 2, 1, 4), (AC, 2, 1, 5), (TO, 2, 0, 4), (TO, 2, 0, 3),
+    (BO, 2, 2, 0), (AC, 2, 0, 7), (BF, 2, 2, 0), (BI, 2, 2, 1), (AC, 2, 1, 7), (BI, 2, 2, 0), (TO, 2, 1, 6),
+    (TO, 2, 0, 6), (TO, 2, 1, 5), (TO, 2, 0, 5), (BA, 2, 2, 0), (BA, 2, 2, 1), (FIN, 2, 1, 0), (FIN, 2, 2, 0),
     (FIN, 2, 0, 0),
 )
 

time: 135 us -> 134 us (level)
  no operation moved by 1% of the time
where the time goes in v7:
time: 134 us
  Pallas kernels  133 us (99%)
  local copies, waits for them, and re-layouts  1.66 us (1%)
    pallas_call x1, Pallas kernels, run_layers(): pl.pallas_call(layers_kernel, out_shape=jax.ShapeDtypeStruct((HALF, 4, 12...  133 us

profile of v7, /device:TPU:1, one launch (start us, length us, event | category | flops | bytes accessed | tf_op | source)
XLA Modules:
  0.0 134.3 jit_solution(2488284431054753352)
XLA Ops:
  0.0 132.7 %shard_map.64 = bf16[128,4,128]{2,1,0:T(4,128)(2,1)} custom-call(bf16[3,4,2,2,8,128,128]{6,5,4,3,2,1,0:T(8,128)(2,1)} %bitcast.3, bf16[128,4,1,128]{3,2,1,0:T(2,128)(2,1)} %bitcast.4, s32[3,1,128]{2,1,0:T(1,128)} %row_in.1, s32[3,1,128]{2,1,0:T(1,128)} %live_in.1, s32[3,1,128]{2,1,0:T(1,128)} %bitcast.5, f32[3,512]{1,0:T(4,128)} %bias.1), custom_call_target="tpu_custom_call" | custom-call | tf_op jit(solution)/shard_map/pallas_call | solution.py:465
  132.7 1.7 %reshape.11 = bf16[1,65536]{1,0:T(2,128)(2,1)} reshape(bf16[128,4,128]{2,1,0:T(4,128)(2,1)} %shard_map.64) | data formatting | bytes 262144 | tf_op jit(solution)/shard_map/reshape | solution.py:480
